TPU v7x, 32 devices: a whole 2x2x4 slice. The times are simulated.
32 devices in a mesh: prow: 4 (over z), pcol: 8 (over y, x, core).
Axes of the slice: x: 2, y: 2, z: 4, core: 2. Of those that a mesh axis runs over, the one named last changes fastest.
Arguments:
- values: float32 [12, 4, 4, 8, 256, 256], P(None, 'prow', None, 'pcol'), may hold values from -6 to 6
- pattern: int32 [12, 4, 4, 8], P(None, 'prow', None, 'pcol'), may hold values from 0 to 1
Outputs:
- factored: float32 [12, 4, 4, 8, 256, 256], P(None, 'prow', None, 'pcol')
All inputs are finite; a program needn't handle non-finite values.
Results may differ from a plain program's by a relative error of at most 0.0003.
Values sent between devices are 32-bit elements; how exact they have to be, the bound alone decides.
No kernel may reach another device: no remote copies, remote signals or barrier semaphores. Data moves between devices by JAX's collectives and lax.ppermute only.
A program may use at most 128 MiB of HBM per device.

v0:
```python
import math

import jax
import jax.numpy as jnp
from jax import lax
from jax.sharding import PartitionSpec as P

SWEEPS = 3


shift_coef = 5.0


def spread(value, axis, source):
    kept = jnp.where(lax.axis_index(axis) == source, value, 0).astype(value.dtype)
    return lax.psum(kept, axis)


def newton(block, shift):
    width = block.shape[0]
    eye = jnp.eye(width, dtype=jnp.float32)
    approx = eye / shift
    for step in range(SWEEPS):
        inner = jnp.dot(block, approx, precision=lax.Precision.HIGHEST)
        approx = jnp.dot(approx, 2.0 * eye - inner, precision=lax.Precision.HIGHEST)
    return approx


def spread_inverse(block, shift, root_row):
    return spread(newton(block, shift), "prow", root_row)


def apply_panel(blocks, rows_g, cols_g, mult, upper, k):
    product = jnp.einsum("rab,cbe->rcae", mult, upper, precision=lax.Precision.HIGHEST)
    below = rows_g > k
    trail = (below[:, None] & (cols_g > k)[None, :])[:, :, None, None]
    store = (below[:, None] & (cols_g == k)[None, :])[:, :, None, None]
    out = jnp.where(trail, blocks - product, blocks)
    return jnp.where(store, mult[:, None], out)


def drop_one(array, index, axis_pos):
    return jnp.concatenate(
        [
            lax.slice_in_dim(array, 0, index, axis=axis_pos),
            lax.slice_in_dim(array, index + 1, array.shape[axis_pos], axis=axis_pos),
        ],
        axis=axis_pos,
    )


def put_one(array, piece, index, axis_pos):
    return jnp.concatenate(
        [lax.slice_in_dim(array, 0, index, axis=axis_pos), piece, array], axis=axis_pos
    )


def factor_panel(column, row, k, shift, nprow, npcol):
    root_row, loc_row = (k % nprow, k // nprow)
    root_col = k % npcol
    inverse = spread_inverse(column[loc_row], shift, root_row)
    mult = jnp.einsum("rab,be->rae", column, inverse, precision=lax.Precision.HIGHEST)
    mult = spread(mult, "pcol", root_col)
    upper = spread(row, "prow", root_row)
    return (mult, upper)


def body(values, pattern):
    rows_loc, cols_loc, width = (values.shape[0], values.shape[2], values.shape[4])
    nprow = lax.axis_size("prow")
    npcol = lax.axis_size("pcol")
    rows_g = jnp.arange(rows_loc, dtype=jnp.int32) * nprow + lax.axis_index("prow")
    cols_g = jnp.arange(cols_loc, dtype=jnp.int32) * npcol + lax.axis_index("pcol")
    shift = shift_coef * math.sqrt(width)
    eye = jnp.eye(width, dtype=jnp.float32)
    blocks = values[:, 0, :, 0] * pattern[:, 0, :, 0].astype(jnp.float32)[:, :, None, None]
    diag = jnp.where(rows_g[:, None] == cols_g[None, :], shift, 0.0).astype(jnp.float32)
    blocks = blocks + diag[:, :, None, None] * eye
    row_first, col_first = (0 // nprow, 0 // npcol)
    row_next, col_next = (1 // nprow, 1 // npcol)
    mult_first, upper_first = factor_panel(
        blocks[:, col_first], blocks[row_first], 0, shift, nprow, npcol
    )
    column = apply_panel(
        blocks[:, col_next : col_next + 1],
        rows_g,
        cols_g[col_next : col_next + 1],
        mult_first,
        upper_first[col_next : col_next + 1],
        0,
    )[:, 0]
    row = apply_panel(
        blocks[row_next : row_next + 1],
        rows_g[row_next : row_next + 1],
        cols_g,
        mult_first[row_next : row_next + 1],
        upper_first,
        0,
    )[0]
    mult_next, upper_next = factor_panel(column, row, 1, shift, nprow, npcol)
    inner = drop_one(drop_one(blocks, row_next, 0), col_next, 1)
    inner = apply_panel(
        inner,
        drop_one(rows_g, row_next, 0),
        drop_one(cols_g, col_next, 0),
        drop_one(mult_first, row_next, 0),
        drop_one(upper_first, col_next, 0),
        0,
    )
    inner = put_one(inner, drop_one(column, row_next, 0)[:, None], col_next, 1)
    blocks = put_one(inner, row[None], row_next, 0)
    blocks = apply_panel(blocks, rows_g, cols_g, mult_next, upper_next, 1)
    return blocks[:, None, :, None]


def solution(mesh):
    placed = (P(None, "prow", None, "pcol", None, None), P(None, "prow", None, "pcol"))
    return jax.shard_map(
        body,
        mesh=mesh,
        in_specs=placed,
        out_specs=P(None, "prow", None, "pcol", None, None),
        check_vma=False,
    )
```

profile of v0, /device:TPU:0, one launch (start us, length us, event | category | flops | bytes accessed | tf_op | source)
XLA Modules:
  0.0 351.3 jit_solution(18210090547723713760)
XLA Ops:
  6.6 0.7 convert_element_type.28
  7.4 12.2 %fusion.2 = f32[12,4,256,256]{3,2,0,1:T(8,128)} fusion(f32[12,1,4,1,256,256]{5,4,3,2,1,0:T(8,128)} %param.2, f32[256,256]{1,0:T(8,128)S(1)} %fusion.29, f32[12,4]{0,1:T(4,128)S(1)} %compare_select_fusion, f32[12,4]{0,1:T(4,128)S(1)} %bitcast.102), kind=kLoop, calls=%fused_computation.5 | loop fusion | flops 9437184 | bytes 25428352 | tf_op jit(solution)/shard_map/add | solution.py:78
  19.6 1.3 convolution_subtract_fusion.5
  21.3 1.3 convolution_subtract_fusion.4
  23.0 1.3 convolution_subtract_fusion.3
  24.4 2.3 select_bitcast_fusion.1
  26.7 1.1 convolution_select_fusion.1
  27.8 62.9 %all-reduce.13.cloned.1.call-done = (f32[256,256]{1,0:T(8,128)}, f32[4,256,256]{2,1,0:T(8,128)}) async-done(((f32[256,256]{1,0:T(8,128)}, f32[4,256,256]{2,1,0:T(8,128)}), (f32[256,256]{1,0:T(8,128)}, f32[4,256,256]{2,1,0:T(8,128)})) %all-reduce.13.cloned.1.call-update) | async-done | bytes 1310736 | tf_op jit(solution)/shard_map/psum | solution.py:16
  90.8 6.2 %fusion.12 = f32[12,256,256]{2,1,0:T(8,128)} fusion(f32[12,4,256,256]{3,2,0,1:T(8,128)} %fusion.2, pred[]{:T(512)S(6)} %eq.84, f32[256,256]{1,0:T(8,128)} %get-tuple-element.7), kind=kOutput, calls=%fused_computation.16 | convolution fusion | flops 2416705536 | bytes 6553601 | tf_op jit(solution)/shard_map/rab,be->rae/dot_general | solution.py:62
  97.4 68.7 %all-reduce.7.cloned.1.call-done = f32[12,256,256]{2,1,0:T(8,128)} async-done(((f32[12,256,256]{2,1,0:T(8,128)}), f32[12,256,256]{2,1,0:T(8,128)}) %all-reduce.7.cloned.1.call-update) | async-done | bytes 3145744 | tf_op jit(solution)/shard_map/psum | solution.py:16
  166.1 6.6 %fusion.4 = f32[12,1,256,256]{3,2,0,1:T(8,128)S(1)} fusion(f32[12,256,256]{2,1,0:T(8,128)} %all-reduce.7.cloned.1.call-done, f32[12,4,256,256]{3,2,0,1:T(8,128)} %fusion.2, pred[12]{0:T(512)(128)(4,1)S(1)} %get-tuple-element.15, pred[12]{0:T(512)(128)(4,1)S(1)} %get-tuple-element.16, f32[4,256,256]{2,1,0:T(8,128)} %get-tuple-element.8), kind=kOutput, calls=%fused_computation.8 | convolution fusion | flops 2418278400 | bytes 12845080 | tf_op jit(solution)/shard_map/rab,cbe->rcae/dot_general | solution.py:34
  173.1 0.4 fusion.20
  174.6 1.1 copy-done.1
  175.7 2.4 fusion.18
  178.1 1.1 copy-done.4
  179.2 1.1 select_bitcast_fusion
  180.3 1.1 convolution_select_fusion
  181.5 60.2 %all-reduce.11.cloned.1.call-done = (f32[256,256]{1,0:T(8,128)}, f32[4,256,256]{2,1,0:T(8,128)}) async-done(((f32[256,256]{1,0:T(8,128)}, f32[4,256,256]{2,1,0:T(8,128)}), (f32[256,256]{1,0:T(8,128)}, f32[4,256,256]{2,1,0:T(8,128)})) %all-reduce.11.cloned.1.call-update) | async-done | bytes 1310736 | tf_op jit(solution)/shard_map/psum | solution.py:16
  241.7 5.3 %fusion.15 = f32[12,256,256]{2,1,0:T(8,128)} fusion(f32[12,1,256,256]{3,2,0,1:T(8,128)S(1)} %fusion.4, pred[]{:T(512)S(6)} %eq.82, f32[256,256]{1,0:T(8,128)} %get-tuple-element.5), kind=kOutput, calls=%fused_computation.17 | convolution fusion | flops 2416705536 | bytes 6553601 | tf_op jit(solution)/shard_map/rab,be->rae/dot_general | solution.py:62
  247.2 1.8 slice-done.1
  249.3 11.9 %fusion.3 = f32[11,3,256,256]{3,2,0,1:T(8,128)} fusion(f32[12,4,256,256]{3,2,0,1:T(8,128)} %fusion.2, f32[11,256,256]{2,1,0:T(8,128)S(1)} %slice-done.1, pred[11,3]{0,1:T(4,128)(4,1)S(1)} %get-tuple-element.12, pred[11,3]{0,1:T(4,128)(4,1)S(1)} %get-tuple-element.11, f32[4,256,256]{2,1,0:T(8,128)S(1)} %copy-done.3), kind=kOutput, calls=%fused_computation.6 | convolution fusion | flops 6650265600 | bytes 23856128 | tf_op jit(solution)/shard_map/rab,cbe->rcae/dot_general | solution.py:34
  261.2 54.8 %all-reduce.9.cloned.1.call-done = f32[12,256,256]{2,1,0:T(8,128)} async-done(((f32[12,256,256]{2,1,0:T(8,128)}), f32[12,256,256]{2,1,0:T(8,128)}) %all-reduce.9.cloned.1.call-update) | async-done | bytes 3145744 | tf_op jit(solution)/shard_map/psum | solution.py:16
  316.0 18.0 %fusion.1 = f32[12,1,4,1,256,256]{5,4,0,2,3,1:T(8,128)} fusion(f32[11,3,256,256]{3,2,0,1:T(8,128)} %fusion.3, f32[11,1,256,256]{3,2,0,1:T(8,128)S(1)} %slice-done, f32[1,4,256,256]{3,2,0,1:T(8,128)} %copy-done.4, f32[12,256,256]{2,1,0:T(8,128)} %all-reduce.9.cloned.1.call-done, pred[12,4]{0,1:T(4,128)(4,1)S(1)} %get-tuple-element.10, ...), kind=kOutput, calls=%fused_computation.3 | convolution fusion | flops 9679405056 | bytes 29360224 | tf_op jit(solution)/shard_map/rab,cbe->rcae/dot_general | solution.py:34
  334.0 10.8 %copy.12 = f32[12,1,4,1,256,256]{5,4,3,2,1,0:T(8,128)} copy(f32[12,1,4,1,256,256]{5,4,0,2,3,1:T(8,128)} %fusion.1) | data formatting | bytes 25165824 | tf_op jit(solution)/shard_map/broadcast_in_dim | solution.py:113
  (38 shorter events, 3.4 us)
Async XLA Ops:
  6.5 84.2 %all-reduce.13.cloned.1.call-start = ((), (), s32[]{:S(2)}) async-start(), calls=%async_computation.3 | async-start | bytes 2621440 | tf_op jit(solution)/shard_map/psum | solution.py:16
  27.8 138.3 %all-reduce.7.cloned.1.call-start = ((), (), s32[]{:S(2)}) async-start(), calls=%async_computation | async-start | bytes 6291456 | tf_op jit(solution)/shard_map/psum | solution.py:16
  97.0 144.7 %all-reduce.11.cloned.1.call-start = ((), (), s32[]{:S(2)}) async-start(), calls=%async_computation.2 | async-start | bytes 2621440 | tf_op jit(solution)/shard_map/psum | solution.py:16
  166.0 9.7 %copy-start.2 = (f32[4,256,256]{2,1,0:T(8,128)S(1)}, f32[4,256,256]{2,1,0:T(8,128)}, u32[]{:S(2)}) copy-start(f32[4,256,256]{2,1,0:T(8,128)} %get-tuple-element.8) | copy-start | bytes 3145732
  172.7 74.5 %copy-start = (f32[12,1,256,256]{3,2,0,1:T(8,128)}, f32[12,1,256,256]{3,2,0,1:T(8,128)S(1)}, u32[]{:S(2)}) copy-start(f32[12,1,256,256]{3,2,0,1:T(8,128)S(1)} %fusion.4) | copy-start | bytes 9437188
  172.7 3.0 copy-start.1
  178.1 1.1 copy-start.4
  181.4 134.6 %all-reduce.9.cloned.1.call-start = ((), (), s32[]{:S(2)}) async-start(), calls=%async_computation.1 | async-start | bytes 6291456 | tf_op jit(solution)/shard_map/psum | solution.py:16
  247.2 1.8 slice-start.1
  247.2 2.1 copy-start.3
  249.3 66.7 %slice-start = ((f32[12,1,256,256]{3,2,0,1:T(8,128)}), f32[11,1,256,256]{3,2,0,1:T(8,128)S(1)}, s32[]{:S(2)}) async-start(f32[12,1,256,256]{3,2,0,1:T(8,128)} %copy-done), calls=%async_computation.4 | async-start | bytes 5767168 | tf_op jit(solution)/shard_map/slice | solution.py:46
Sparse Core Ops, SparseCore 0:
  27.9 62.8 all-reduce.12
  97.1 68.8 all-reduce.6
  181.5 60.1 all-reduce.10
  247.1 68.8 all-reduce.8
where the time goes:
time: 352 us; the launch traced here: 351 us
  waiting for transfers between devices  247 us (70%)
  matrix products  59.1 us (17%)
  other arithmetic  16.7 us (5%)
  local copies, waits for them, and re-layouts  15 us (4%)
  between operations  13.4 us (4%)
    psum x4, waiting for transfers between devices, spread(): return lax.psum(kept, axis)  247 us
    dot_general x4, matrix products, apply_panel(): jnp.einsum('rab,cbe->rcae', mult, upper, precision=lax.Precision.HIGHEST)  38.8 us
    add x1, other arithmetic, body(): blocks = blocks + diag[:, :, None, None] * eye  12.2 us
    dot_general x2, matrix products, factor_panel(): jnp.einsum('rab,be->rae', column, inverse, precision=lax.Precision.HIGHEST)  11.5 us
    broadcast_in_dim x1, local copies, waits for them, and re-layouts, body(): return blocks[:, None, :, None]  10.8 us
  transfers between devices with their start and end apart: 4, of which 4 were waited for; matrix products, arithmetic and copies ran while one was open for 3% of the time, Pallas kernels for 0%

commit v1 on v0

v1 whole, which is shorter than its diff:
```python
import functools
import math

import jax
import jax.numpy as jnp
from jax import lax
from jax.experimental import pallas as pl
from jax.experimental.pallas import tpu as pltpu
from jax.sharding import PartitionSpec as P


SWEEPS = 3

shift_coef = 5.0


def split(x):
    high = x.astype(jnp.bfloat16)
    return high, (x - high.astype(jnp.float32)).astype(jnp.bfloat16)


def dot3(a, b):
    mul = functools.partial(jnp.dot, preferred_element_type=jnp.float32)
    return mul(a[0], b[0]) + mul(a[0], b[1]) + mul(a[1], b[0])


def identity(width):
    row = lax.broadcasted_iota(jnp.int32, (width, width), 0)
    col = lax.broadcasted_iota(jnp.int32, (width, width), 1)
    return jnp.where(row == col, 1.0, 0.0).astype(jnp.float32)


def newton(block, shift, eye):
    error = eye - block * (1.0 / shift)
    approx = (eye + error) * (1.0 / shift)
    for _ in range(1, SWEEPS):
        parts = split(error)
        error = dot3(parts, parts)
        approx = approx + dot3(split(approx), split(error))
    return approx


def pivot_blocks(shift, first, mine, other, out):
    width = mine.shape[1]
    eye = identity(width)
    a00 = jnp.where(first, mine[0], other[0])
    a10 = jnp.where(first, mine[1], other[1])
    a01 = jnp.where(first, other[0], mine[0])
    a11 = jnp.where(first, other[1], mine[1])
    x0 = newton(a00, shift, eye)
    x0s = split(x0)
    a01s = split(a01)
    t1 = dot3(split(a10), x0s)
    z = dot3(x0s, a01s)
    t1s, zs = split(t1), split(z)
    x1 = newton(a11 - dot3(t1s, a01s), shift, eye)
    x1s = split(x1)
    k10 = dot3(x1s, t1s)
    out[0] = x0 + dot3(zs, split(k10))
    out[1] = -dot3(zs, x1s)
    out[2] = -k10
    out[3] = x1
    out[4] = t1
    out[5] = x0


def factor_kernel(shift, plan, place, mine_in, other_in, *refs):
    right, row_one, blocks, upper, pivot, sems, upper_sems = refs[-7:]
    ncols, width = upper.shape[0] // 2, upper.shape[2]
    pcol, core = place[1], place[2]
    near = [pltpu.make_async_copy(mine_in, blocks.at[0], sems.at[0]), pltpu.make_async_copy(other_in, blocks.at[1], sems.at[1])]
    for copy in near:
        copy.start()
    picked_copies(plan, place, refs[:-7], upper, upper_sems, False)
    for copy in near:
        copy.wait()
    pivot_blocks(shift, core == 0, blocks.at[0], blocks.at[1], pivot)
    picked_copies(plan, place, refs[:-7], upper, upper_sems, True)
    w = [split(pivot[n]) for n in range(5)]
    for c in range(ncols):
        cols = slice(c * width, (c + 1) * width)
        u0, u1 = split(upper[c]), split(upper[ncols + c])
        g0 = dot3(w[0], u0) + dot3(w[1], u1)
        g1 = dot3(w[2], u0) + dot3(w[3], u1)
        one = upper[ncols + c] - dot3(w[4], u0)
        if c == 0:
            g0 = jnp.where(pcol == 0, -pivot[5], jnp.where(pcol == 1, -pivot[1], g0))
            g1 = jnp.where(pcol == 0, 0.0, jnp.where(pcol == 1, -pivot[3], g1))
            one = jnp.where(pcol == 0, pivot[4], one)
        row_one[c] = one
        near = split(jnp.where(core == 0, g0, g1))
        far = split(jnp.where(core == 0, g1, g0))
        for n, piece in enumerate((near[0], far[0], near[1], far[1], near[0], far[0])):
            right[n * width:(n + 1) * width, cols] = piece


def update_kernel(sizes, shift, place, pattern, values, mine_a, mine_b, other_a, other_b, right, one, *rest):
    nprow, npcol, half, count, base, ncols, width = sizes
    out, blocks, sides, left, sems, side_sems, out_sems = rest[-7:]
    prow, pcol, core = place[0], place[1], place[2]

    def row0(part):
        return jnp.where(part == 0, core, 1 - core) * half + base

    def fetch(n):
        c, part = n // 2, n % 2
        return pltpu.make_async_copy(values.at[pl.ds(row0(part), count), c], blocks.at[n], sems.at[n])

    def store(n):
        c, part = n // 2, n % 2
        return pltpu.make_async_copy(blocks.at[n], out.at[pl.ds(row0(part), count), c], out_sems.at[n])

    def fetch_all(c):
        fetch(2 * c).start()
        fetch(2 * c + 1).start()

    sources = [pltpu.make_async_copy(ref, sides.at[n], side_sems.at[n]) for n, ref in enumerate((other_b, other_a))]
    for copy in sources:
        copy.start()
    for c in range(min(2, ncols)):
        fetch_all(c)
    for part, (near, far) in enumerate(((mine_a, mine_b), (sides.at[0], sides.at[1]))):
        if part == 1:
            for copy in sources:
                copy.wait()
        near_high, near_low = split(near[...].reshape(count * width, width))
        far_high, far_low = split(far[...].reshape(count * width, width))
        rows = slice(part * count * width, (part + 1) * count * width)
        for k, piece in enumerate((near_high, far_high, near_high, far_high, near_low, far_low)):
            left[rows, k * width:(k + 1) * width] = piece
    for c in range(ncols):
        if c + 2 < ncols:
            fetch_all(c + 2)
        cols = slice(c * width, (c + 1) * width)
        product = jnp.dot(left[...], right[:, cols], preferred_element_type=jnp.float32)
        for part in range(2):
            n = 2 * c + part
            fetch(n).wait()
            first = row0(part)
            for r in range(count):
                keep = pattern[first + r, c].astype(jnp.float32)
                if c == 0:
                    keep = jnp.where((pcol < 2) & ((first + r > 0) | (prow > 0)), 0.0, keep)
                at = (part * count + r) * width
                change = product[at:at + width]
                if base == 0 and r == 0:
                    change = jnp.where((first == 0) & (prow == 0), 0.0, change)
                blocks[n, r] = blocks[n, r] * keep - change
            for r in range(count):
                row_g = (first + r) * nprow + prow

                @pl.when((row_g == c * npcol + pcol) & (row_g != 1))
                def _():
                    blocks[n, r] = blocks[n, r] + shift * identity(width)

            if base == 0:
                @pl.when((first == 0) & (prow == 1))
                def _():
                    blocks[n, 0] = one[c]

            store(n).start()
    for n in range(2 * ncols):
        store(n).wait()


def rows_kernel(sizes, shift, place, pattern, values, whole, *parts):
    npcol, starts = sizes
    prow, pcol = place[0], place[1]
    ncols, width = values.shape[1], values.shape[2]
    for c in range(ncols):
        on = jnp.where(c * npcol + pcol == prow, shift, 0.0)
        block = values[0, c] * pattern[0, c].astype(jnp.float32) + on * identity(width)
        whole[c] = block
        n = max(n for n in range(len(starts)) if starts[n] <= c)
        parts[n][c - starts[n]] = block


def cols_kernel(sizes, shift, place, pattern, near, far, *parts):
    nprow, half, cut = sizes
    prow, pcol, core = place[0], place[1], place[2]
    width = near.shape[2]
    for owner, source, pieces in ((1 - core, far, parts[0:2]), (core, near, parts[2:4])):
        for r in range(half):
            row = owner * half + r
            block = source[r, 0] * pattern[row, 0].astype(jnp.float32)
            if r == 0:
                block = block + jnp.where(row * nprow + prow == pcol, shift, 0.0) * identity(width)
            pieces[r >= cut][r - cut * (r >= cut)] = block


def picked_copies(plan, place, refs, out, sems, wait):
    at = 0
    for n, (entry, start, count, offsets) in enumerate(plan):
        for k, offset in enumerate(offsets):
            source = refs[at + k].at[pl.ds(offset, count)]

            @pl.when(place[entry] == k)
            def _():
                copy = pltpu.make_async_copy(source, out.at[pl.ds(start, count)], sems.at[n])
                copy.wait() if wait else copy.start()
        at += len(offsets)


def pick_kernel(plan, place, *refs):
    for wait in (False, True):
        picked_copies(plan, place, refs[:-2], refs[-2], refs[-1], wait)


def pick_plan(groups):
    start, plan, operands = 0, [], []
    for entry, count, candidates in groups:
        plan.append((entry, start, count, tuple(offset for _, offset in candidates)))
        operands += [array for array, _ in candidates]
        start += count
    return tuple(plan), operands, start


def pick(place, groups):
    plan, operands, total = pick_plan(groups)
    return pl.pallas_call(
        functools.partial(pick_kernel, plan),
        out_shape=jax.ShapeDtypeStruct((total,) + operands[0].shape[1:], jnp.float32),
        in_specs=[pl.BlockSpec(memory_space=pltpu.SMEM)] + [pl.BlockSpec(memory_space=pl.ANY)] * len(operands),
        out_specs=pl.BlockSpec(memory_space=pltpu.VMEM),
        scratch_shapes=[pltpu.SemaphoreType.DMA((len(plan),))],
        name="pick",
    )(place, *operands)


def ring_of(chips):
    return [0] + list(range(1, chips, 2)) + list(range((chips - 1) // 2 * 2, 0, -2))


def choose(index, options):
    out = options[0]
    for n in range(1, len(options)):
        out = jnp.where(index == n, options[n], out)
    return out


def body(values, pattern):
    nrows, ncols, width = values.shape[0], values.shape[2], values.shape[4]
    nprow, npcol = lax.axis_size("prow"), lax.axis_size("pcol")
    chips = npcol // 2
    half = nrows // 2
    cut = half // 2
    prow, pcol = lax.axis_index("prow"), lax.axis_index("pcol")
    core = pcol % 2
    shift = shift_coef * math.sqrt(width)
    vals, pat = values[:, 0, :, 0], pattern[:, 0, :, 0]
    ring = ring_of(chips)
    rings = [ring, [ring[0]] + ring[:0:-1]]
    spot = sum(jnp.where(pcol // 2 == c, jnp.where(core == 0, rings[0].index(c), rings[1].index(c)), 0) for c in range(chips))
    place = jnp.stack([prow, pcol, core, spot]).astype(jnp.int32)
    smem = pl.BlockSpec(memory_space=pltpu.SMEM)
    vmem = pl.BlockSpec(memory_space=pltpu.VMEM)
    array = lambda *shape: jax.ShapeDtypeStruct(shape + (width, width), jnp.float32)
    full = lambda *shape: pl.BlockSpec(shape + (width, width), lambda *_: (0,) * (len(shape) + 2))

    counts = [1, 1, ncols - 2] if ncols > 2 else [1] * ncols
    starts = [sum(counts[:n]) for n in range(len(counts))]
    rows = pl.pallas_call(
        functools.partial(rows_kernel, (npcol, tuple(starts)), shift),
        out_shape=[array(ncols)] + [array(count) for count in counts],
        grid_spec=pltpu.PrefetchScalarGridSpec(
            num_scalar_prefetch=2, grid=(1,),
            in_specs=[full(1, ncols)],
            out_specs=[full(ncols)] + [full(count) for count in counts],
        ),
        name="rows",
    )(place, pat, vals)
    cols = pl.pallas_call(
        functools.partial(cols_kernel, (nprow, half, cut), shift),
        out_shape=[array(cut), array(half - cut)] * 2,
        grid_spec=pltpu.PrefetchScalarGridSpec(
            num_scalar_prefetch=2, grid=(1,),
            in_specs=[
                pl.BlockSpec((half, 1, width, width), lambda _, place, pat: (place[2], 0, 0, 0)),
                pl.BlockSpec((half, 1, width, width), lambda _, place, pat: (1 - place[2], 0, 0, 0)),
            ],
            out_specs=[full(cut), full(half - cut)] * 2,
        ),
        name="cols",
    )(place, pat, vals, vals)

    back = lax.ppermute(rows[0], "prow", [(1, 0)])
    upper0, upper1 = [], []
    for n, (start, count) in enumerate(zip(starts, counts)):
        hops = [rows[1 + n]]
        for hop in range(1, nprow):
            pairs = [(hop - 1, hop)] + ([(hop, hop + 1)] if hop + 1 < nprow else [])
            hops.append(lax.ppermute(hops[-1], "prow", pairs))
        upper0.append((0, count, [(hop, 0) for hop in hops]))
        upper1.append((0, count, [(back, start)] + [(hop, 0) for hop in hops[:-1]]))
    pivots = pick(place, [upper0[0], upper1[0]])

    swap_pairs = [(q, q ^ 1) for q in range(npcol)]
    crossed = []
    for n in range(2):
        crossed.append(lax.ppermute(cols[n], "pcol", swap_pairs))
    sent = [cols[2], crossed[0], cols[3], pivots, crossed[1]]
    got = []
    for chunk in sent:
        hops = [chunk]
        for hop in range(1, chips):
            pairs = [(2 * way[hop - 1] + b, 2 * way[hop] + b) for b, way in enumerate(rings)]
            hops.append(lax.ppermute(hops[-1], "pcol", pairs))
        got.append(choose(spot, hops))
    swapped = []
    for chunk in got:
        swapped.append(lax.ppermute(chunk, "pcol", swap_pairs))

    anywhere = pl.BlockSpec(memory_space=pl.ANY)
    plan, operands, _ = pick_plan(upper0 + upper1)
    right, row_one = pl.pallas_call(
        functools.partial(factor_kernel, shift, plan),
        out_shape=[jax.ShapeDtypeStruct((6 * width, ncols * width), jnp.bfloat16), array(ncols)],
        in_specs=[smem] + [anywhere] * (2 + len(operands)),
        out_specs=[vmem, vmem],
        scratch_shapes=[
            pltpu.VMEM((2, 2, width, width), jnp.float32),
            pltpu.VMEM((2 * ncols, width, width), jnp.float32),
            pltpu.VMEM((6, width, width), jnp.float32),
            pltpu.SemaphoreType.DMA((2,)),
            pltpu.SemaphoreType.DMA((len(plan),)),
        ],
        compiler_params=pltpu.CompilerParams(vmem_limit_bytes=24 * 1024 * 1024),
        name="factor",
    )(place, got[3], swapped[3], *operands)

    out = None
    for base, count, a, b in [(0, cut, 0, 1), (cut, half - cut, 2, 4)]:
        carried = [] if out is None else [out]
        out = pl.pallas_call(
            functools.partial(update_kernel, (nprow, npcol, half, count, base, ncols, width), shift),
            out_shape=jax.ShapeDtypeStruct(vals.shape, jnp.float32),
            in_specs=[smem, smem, anywhere, vmem, vmem, anywhere, anywhere, vmem, vmem] + [anywhere] * len(carried),
            out_specs=anywhere,
            scratch_shapes=[
                pltpu.VMEM((2 * ncols, count, width, width), jnp.float32),
                pltpu.VMEM((2, count, width, width), jnp.float32),
                pltpu.VMEM((2 * count * width, 6 * width), jnp.bfloat16),
                pltpu.SemaphoreType.DMA((2 * ncols,)),
                pltpu.SemaphoreType.DMA((2,)),
                pltpu.SemaphoreType.DMA((2 * ncols,)),
            ],
            input_output_aliases={9: 0} if carried else {},
            compiler_params=pltpu.CompilerParams(vmem_limit_bytes=40 * 1024 * 1024),
        )(place, pat, vals, got[a], got[b], swapped[a], swapped[b], right, row_one, *carried)
    return out[:, None, :, None]


def solution(mesh):
    placed = (P(None, "prow", None, "pcol", None, None), P(None, "prow", None, "pcol"))
    return jax.shard_map(
        body,
        mesh=mesh,
        in_specs=placed,
        out_specs=P(None, "prow", None, "pcol", None, None),
        check_vma=False,
    )
```

time: 352 us -> 156 us (0.44)
  the two profiles are of different devices: /device:TPU:0 before, /device:TPU:25 now
where the time goes in v1:
time: 156 us; the launch traced here: 155 us
  starting transfers between devices  54.2 us (35%)
  waiting for transfers between devices  47.4 us (30%)
  Pallas kernels  44.3 us (28%)
  other arithmetic  6.18 us (4%)
  local copies, waits for them, and re-layouts  2.12 us (1%)
    ppermute x15, starting transfers between devices, body(): hops.append(lax.ppermute(hops[-1], 'pcol', pairs))  31.6 us
    pallas_call x2, Pallas kernels, body(): pl.pallas_call(functools.partial(update_kernel, (nprow, npcol, half, coun...  27.2 us
    ppermute x9, waiting for transfers between devices, body(): hops.append(lax.ppermute(hops[-1], 'prow', pairs))  26.6 us
    ppermute x15, waiting for transfers between devices, body(): hops.append(lax.ppermute(hops[-1], 'pcol', pairs))  19.3 us
    ppermute x5, starting transfers between devices, body(): swapped.append(lax.ppermute(chunk, 'pcol', swap_pairs))  11.2 us
    ppermute x9, starting transfers between devices, body(): hops.append(lax.ppermute(hops[-1], 'prow', pairs))  9.86 us
    pallas_call x1, Pallas kernels, body(): pl.pallas_call(functools.partial(factor_kernel, shift, plan), out_shape=[...  6.77 us
    select_n x5, other arithmetic, choose(): out = jnp.where(index == n, options[n], out)  5.6 us
  transfers between devices with their start and end apart: 32, of which 10 were waited for; matrix products, arithmetic and copies ran while one was open for 4% of the time, Pallas kernels for 18%

profile of v1, /device:TPU:25, one launch (start us, length us, event | category | flops | bytes accessed | tf_op | source)
XLA Modules:
  0.0 154.8 jit_solution(11169839761547820578)
XLA Ops:
  1.9 3.4 %rows.1 = (f32[4,256,256]{2,1,0:T(8,128)}, f32[1,256,256]{2,1,0:T(8,128)}, f32[1,256,256]{2,1,0:T(8,128)}, f32[2,256,256]{2,1,0:T(8,128)}) custom-call(s32[4]{0:T(128)} %pad_add_fusion.place, s32[12,4]{1,0:T(8,128)} %copy.7.pattern, f32[12,4,256,256]{3,2,1,0:T(8,128)} %bitcast.9), custom_call_target="tpu_custom_call" | custom-call | tf_op jit(solution)/shard_map/rows/pallas_call | solution.py:262
  8.2 4.4 %cols.1 = (f32[3,256,256]{2,1,0:T(8,128)}, f32[3,256,256]{2,1,0:T(8,128)}, f32[3,256,256]{2,1,0:T(8,128)}, f32[3,256,256]{2,1,0:T(8,128)}) custom-call(s32[4]{0:T(128)} %pad_add_fusion.place, s32[12,4]{1,0:T(8,128)} %copy.7.pattern, f32[12,4,256,256]{3,2,1,0:T(8,128)} %bitcast.10, f32[12,4,256,256]{3,2,1,0:T(8,128)} %bitcast.11), custom_call_target="tpu_custom_call" | custom-call | tf_op jit(solution)/shard_map/cols/pallas_call | solution.py:272
  15.3 3.2 %collective-permute-start = (f32[3,256,256]{2,1,0:T(8,128)}, f32[3,256,256]{2,1,0:T(8,128)S(1)}, u32[]{:S(2)}, u32[]{:S(2)}) collective-permute-start(f32[3,256,256]{2,1,0:T(8,128)} %get-tuple-element.15), channel_id=1, source_target_pairs={{0,2},{1,5},{8,10},{9,13},{16,18},{17,21},{24,26},{25,29}} | collective-permute-start | bytes 2359304 | tf_op jit(solution)/shard_map/ppermute | solution.py:307
  18.5 1.9 %collective-permute-done.10.refs_2_.refs_7_.refs_15_ = f32[1,256,256]{2,1,0:T(8,128)S(1)} collective-permute-done((f32[1,256,256]{2,1,0:T(8,128)S(1)}, f32[1,256,256]{2,1,0:T(8,128)S(1)}, u32[]{:S(2)}, u32[]{:S(2)}) %collective-permute-start.10) | collective-permute-done | bytes 262176 | tf_op jit(solution)/shard_map/ppermute | solution.py:292
  21.7 10.4 %collective-permute-done.18.refs_6_.refs_19_ = f32[1,256,256]{2,1,0:T(8,128)S(1)} collective-permute-done((f32[1,256,256]{2,1,0:T(8,128)S(1)}, f32[1,256,256]{2,1,0:T(8,128)S(1)}, u32[]{:S(2)}, u32[]{:S(2)}) %collective-permute-start.18) | collective-permute-done | bytes 262176 | tf_op jit(solution)/shard_map/ppermute | solution.py:292
  32.9 4.7 %collective-permute-done.11.refs_3_ = f32[1,256,256]{2,1,0:T(8,128)S(1)} collective-permute-done((f32[1,256,256]{2,1,0:T(8,128)S(1)}, f32[1,256,256]{2,1,0:T(8,128)S(1)}, u32[]{:S(2)}, u32[]{:S(2)}) %collective-permute-start.11) | collective-permute-done | bytes 262176 | tf_op jit(solution)/shard_map/ppermute | solution.py:292
  37.6 4.2 %collective-permute-start.23 = (f32[3,256,256]{2,1,0:T(8,128)}, f32[3,256,256]{2,1,0:T(8,128)}, u32[]{:S(2)}, u32[]{:S(2)}) collective-permute-start(f32[3,256,256]{2,1,0:T(8,128)} %get-tuple-element.23), channel_id=1, source_target_pairs={{0,2},{1,5},{8,10},{9,13},{16,18},{17,21},{24,26},{25,29}} | collective-permute-start | bytes 2359304 | tf_op jit(solution)/shard_map/ppermute | solution.py:307
  41.8 2.2 %collective-permute-start.4 = (f32[3,256,256]{2,1,0:T(8,128)S(1)}, f32[3,256,256]{2,1,0:T(8,128)}, u32[]{:S(2)}, u32[]{:S(2)}) collective-permute-start(f32[3,256,256]{2,1,0:T(8,128)S(1)} %collective-permute-done.3), channel_id=1, source_target_pairs={{0,2},{1,5},{8,10},{9,13},{16,18},{17,21},{24,26},{25,29}} | collective-permute-start | bytes 2359304 | tf_op jit(solution)/shard_map/ppermute | solution.py:307
  44.0 2.2 %collective-permute-start.27 = (f32[3,256,256]{2,1,0:T(8,128)S(1)}, f32[3,256,256]{2,1,0:T(8,128)}, u32[]{:S(2)}, u32[]{:S(2)}) collective-permute-start(f32[3,256,256]{2,1,0:T(8,128)S(1)} %collective-permute-done.26), channel_id=1, source_target_pairs={{0,2},{1,5},{8,10},{9,13},{16,18},{17,21},{24,26},{25,29}} | collective-permute-start | bytes 2359304 | tf_op jit(solution)/shard_map/ppermute | solution.py:307
  47.8 2.3 %collective-permute-done.23 = f32[3,256,256]{2,1,0:T(8,128)} collective-permute-done((f32[3,256,256]{2,1,0:T(8,128)}, f32[3,256,256]{2,1,0:T(8,128)}, u32[]{:S(2)}, u32[]{:S(2)}) %collective-permute-start.23) | collective-permute-done | bytes 786464 | tf_op jit(solution)/shard_map/ppermute | solution.py:307
  50.9 1.6 %collective-permute-start.24 = (f32[3,256,256]{2,1,0:T(8,128)}, f32[3,256,256]{2,1,0:T(8,128)}, u32[]{:S(2)}, u32[]{:S(2)}) collective-permute-start(f32[3,256,256]{2,1,0:T(8,128)} %collective-permute-done.23), channel_id=1, source_target_pairs={{2,6},{5,7},{10,14},{13,15},{18,22},{21,23},{26,30},{29,31}} | collective-permute-start | bytes 2359304 | tf_op jit(solution)/shard_map/ppermute | solution.py:307
  52.5 6.0 %collective-permute-done.4 = f32[3,256,256]{2,1,0:T(8,128)} collective-permute-done((f32[3,256,256]{2,1,0:T(8,128)S(1)}, f32[3,256,256]{2,1,0:T(8,128)}, u32[]{:S(2)}, u32[]{:S(2)}) %collective-permute-start.4) | collective-permute-done | bytes 786464 | tf_op jit(solution)/shard_map/ppermute | solution.py:307
  60.0 6.9 %collective-permute-done.27 = f32[3,256,256]{2,1,0:T(8,128)} collective-permute-done((f32[3,256,256]{2,1,0:T(8,128)S(1)}, f32[3,256,256]{2,1,0:T(8,128)}, u32[]{:S(2)}, u32[]{:S(2)}) %collective-permute-start.27) | collective-permute-done | bytes 786464 | tf_op jit(solution)/shard_map/ppermute | solution.py:307
  70.0 2.5 %pick.1 = f32[2,256,256]{2,1,0:T(8,128)} custom-call(s32[4]{0:T(128)} %pad_add_fusion.place, f32[1,256,256]{2,1,0:T(8,128)} %get-tuple-element.17.refs_0_.refs_5_.refs_13_, f32[1,256,256]{2,1,0:T(8,128)} %copy-done.3, f32[1,256,256]{2,1,0:T(8,128)} %copy-done.5, f32[1,256,256]{2,1,0:T(8,128)} %copy-done.13, f32[4,256,256]{2,1,0:T(8,128)} %copy-done, ...), custom_call_target="tpu_custom_call" | custom-call | tf_op jit(solution)/shard_map/pick/pallas_call | solution.py:220
  72.6 5.8 %collective-permute-start.13 = (f32[2,256,256]{2,1,0:T(8,128)}, f32[2,256,256]{2,1,0:T(8,128)}, u32[]{:S(2)}, u32[]{:S(2)}) collective-permute-start(f32[2,256,256]{2,1,0:T(8,128)} %pick.1), channel_id=1, source_target_pairs={{0,2},{1,5},{8,10},{9,13},{16,18},{17,21},{24,26},{25,29}} | collective-permute-start | bytes 1572872 | tf_op jit(solution)/shard_map/ppermute | solution.py:307
  80.0 4.0 %collective-permute-done.13 = f32[2,256,256]{2,1,0:T(8,128)} collective-permute-done((f32[2,256,256]{2,1,0:T(8,128)}, f32[2,256,256]{2,1,0:T(8,128)}, u32[]{:S(2)}, u32[]{:S(2)}) %collective-permute-start.13) | collective-permute-done | bytes 524320 | tf_op jit(solution)/shard_map/ppermute | solution.py:307
  90.6 6.4 %collective-permute-done.21.refs_10_.refs_23_ = f32[2,256,256]{2,1,0:T(8,128)S(1)} collective-permute-done((f32[2,256,256]{2,1,0:T(8,128)S(1)}, f32[2,256,256]{2,1,0:T(8,128)S(1)}, u32[]{:S(2)}, u32[]{:S(2)}) %collective-permute-start.21) | collective-permute-done | bytes 524320 | tf_op jit(solution)/shard_map/ppermute | solution.py:292
  101.6 3.3 %collective-permute-start.7 = (f32[3,256,256]{2,1,0:T(8,128)S(1)}, f32[3,256,256]{2,1,0:T(8,128)S(1)}, u32[]{:S(2)}, u32[]{:S(2)}) collective-permute-start(f32[3,256,256]{2,1,0:T(8,128)S(1)} %select_select_fusion.3.mine_a), channel_id=1, source_target_pairs={{0,1},{1,0},{2,3},{3,2},{4,5},{5,4},{6,7},{7,6},{8,9},{9,8},{10,11... | collective-permute-start | bytes 2359304 | tf_op jit(solution)/shard_map/ppermute | solution.py:311
  107.8 3.7 %collective-permute-start.8 = (f32[3,256,256]{2,1,0:T(8,128)S(1)}, f32[3,256,256]{2,1,0:T(8,128)S(1)}, u32[]{:S(2)}, u32[]{:S(2)}) collective-permute-start(f32[3,256,256]{2,1,0:T(8,128)S(1)} %select_select_fusion.2.mine_b), channel_id=1, source_target_pairs={{0,1},{1,0},{2,3},{3,2},{4,5},{5,4},{6,7},{7,6},{8,9},{9,8},{10,11... | collective-permute-start | bytes 2359304 | tf_op jit(solution)/shard_map/ppermute | solution.py:311
  111.7 3.2 %collective-permute-done.22.refs_11_ = f32[2,256,256]{2,1,0:T(8,128)S(1)} collective-permute-done((f32[2,256,256]{2,1,0:T(8,128)S(1)}, f32[2,256,256]{2,1,0:T(8,128)S(1)}, u32[]{:S(2)}, u32[]{:S(2)}) %collective-permute-start.22) | collective-permute-done | bytes 524320 | tf_op jit(solution)/shard_map/ppermute | solution.py:292
  114.9 4.1 %collective-permute-start.16 = (f32[2,256,256]{2,1,0:T(8,128)S(1)}, f32[2,256,256]{2,1,0:T(8,128)S(1)}, u32[]{:S(2)}, u32[]{:S(2)}) collective-permute-start(f32[2,256,256]{2,1,0:T(8,128)S(1)} %select_select_fusion.4.mine_in), channel_id=1, source_target_pairs={{0,1},{1,0},{2,3},{3,2},{4,5},{5,4},{6,7},{7,6},{8,9},{9,8},{10,11... | collective-permute-start | bytes 1572872 | tf_op jit(solution)/shard_map/ppermute | solution.py:311
  120.6 6.8 %factor.1 = (bf16[1536,1024]{1,0:T(8,128)(2,1)S(1)}, f32[4,256,256]{2,1,0:T(8,128)S(1)}) custom-call(s32[4]{0:T(128)S(1)} %copy-done.16, f32[2,256,256]{2,1,0:T(8,128)S(1)} %select_select_fusion.4.mine_in, f32[2,256,256]{2,1,0:T(8,128)S(1)} %collective-permute-done.16.other_in, f32[1,256,256]{2,1,0:T(8,128)S(1)} %copy-done.2, f32[1,256,256]{2,1,0:T(8,128)S(1)} %copy-done.4, ...), custom_call_target="tpu_custom_call" | custom-call | tf_op jit(solution)/shard_map/factor/pallas_call | solution.py:315
  127.4 13.6 %shard_map.28.rest_0_ = f32[12,4,256,256]{3,2,1,0:T(8,128)} custom-call(s32[4]{0:T(128)S(1)} %copy-done.16, s32[12,4]{1,0:T(8,128)S(1)} %copy-done.15, f32[12,4,256,256]{3,2,1,0:T(8,128)} %bitcast.12, f32[3,256,256]{2,1,0:T(8,128)S(1)} %select_select_fusion.1.mine_a, f32[3,256,256]{2,1,0:T(8,128)S(1)} %select_select_fusion.mine_b, ...), custom_call_target="tpu_custom_call" | custom-call | tf_op jit(solution)/shard_map/pallas_call | solution.py:334
  141.0 13.6 %shard_map.29 = f32[12,4,256,256]{3,2,1,0:T(8,128)} custom-call(s32[4]{0:T(128)S(1)} %copy-done.16, s32[12,4]{1,0:T(8,128)S(1)} %copy-done.15, f32[12,4,256,256]{3,2,1,0:T(8,128)} %bitcast.13, f32[3,256,256]{2,1,0:T(8,128)S(1)} %select_select_fusion.3.mine_a, f32[3,256,256]{2,1,0:T(8,128)S(1)} %select_select_fusion.2.mine_b, ...), custom_call_target="tpu_custom_call", output_to_operand_aliasing={{}: (9, {})} | custom-call | tf_op jit(solution)/shard_map/pallas_call | solution.py:334
  (95 shorter events, 33.8 us)
Async XLA Ops:
  6.9 13.6 %collective-permute-start.10 = (f32[1,256,256]{2,1,0:T(8,128)S(1)}, f32[1,256,256]{2,1,0:T(8,128)S(1)}, u32[]{:S(2)}, u32[]{:S(2)}) collective-permute-start(f32[1,256,256]{2,1,0:T(8,128)S(1)} %collective-permute-done.9.refs_1_.refs_6_.refs_14_), channel_id=1, source_target_pairs={{8,16},{16,24},{9,17},{17,25},{10,18},{18,26},{11,19},{19,27},{12,... | collective-permute-start | bytes 786440 | tf_op jit(solution)/shard_map/ppermute | solution.py:292
  12.5 29.3 %collective-permute-start.3 = (f32[3,256,256]{2,1,0:T(8,128)}, f32[3,256,256]{2,1,0:T(8,128)S(1)}, u32[]{:S(2)}, u32[]{:S(2)}) collective-permute-start(f32[3,256,256]{2,1,0:T(8,128)} %get-tuple-element.16), channel_id=1, source_target_pairs={{0,1},{1,0},{2,3},{3,2},{4,5},{5,4},{6,7},{7,6},{8,9},{9,8},{10,11... | collective-permute-start | bytes 2359304 | tf_op jit(solution)/shard_map/ppermute | solution.py:300
  13.2 19.0 %collective-permute-start.18 = (f32[1,256,256]{2,1,0:T(8,128)S(1)}, f32[1,256,256]{2,1,0:T(8,128)S(1)}, u32[]{:S(2)}, u32[]{:S(2)}) collective-permute-start(f32[1,256,256]{2,1,0:T(8,128)S(1)} %collective-permute-done.17.refs_5_.refs_18_), channel_id=1, source_target_pairs={{8,16},{16,24},{9,17},{17,25},{10,18},{18,26},{11,19},{19,27},{12,... | collective-permute-start | bytes 786440 | tf_op jit(solution)/shard_map/ppermute | solution.py:292
  15.2 28.8 %collective-permute-start.26 = (f32[3,256,256]{2,1,0:T(8,128)}, f32[3,256,256]{2,1,0:T(8,128)S(1)}, u32[]{:S(2)}, u32[]{:S(2)}) collective-permute-start(f32[3,256,256]{2,1,0:T(8,128)} %get-tuple-element.24), channel_id=1, source_target_pairs={{0,1},{1,0},{2,3},{3,2},{4,5},{5,4},{6,7},{7,6},{8,9},{9,8},{10,11... | collective-permute-start | bytes 2359304 | tf_op jit(solution)/shard_map/ppermute | solution.py:300
  15.3 30.8 %collective-permute-start = (f32[3,256,256]{2,1,0:T(8,128)}, f32[3,256,256]{2,1,0:T(8,128)S(1)}, u32[]{:S(2)}, u32[]{:S(2)}) collective-permute-start(f32[3,256,256]{2,1,0:T(8,128)} %get-tuple-element.15), channel_id=1, source_target_pairs={{0,2},{1,5},{8,10},{9,13},{16,18},{17,21},{24,26},{25,29}} | collective-permute-start | bytes 2359304 | tf_op jit(solution)/shard_map/ppermute | solution.py:307
  20.4 17.1 %collective-permute-start.11 = (f32[1,256,256]{2,1,0:T(8,128)S(1)}, f32[1,256,256]{2,1,0:T(8,128)S(1)}, u32[]{:S(2)}, u32[]{:S(2)}) collective-permute-start(f32[1,256,256]{2,1,0:T(8,128)S(1)} %collective-permute-done.10.refs_2_.refs_7_.refs_15_), channel_id=1, source_target_pairs={{16,24},{17,25},{18,26},{19,27},{20,28},{21,29},{22,30},{23,31}} | collective-permute-start | bytes 786440 | tf_op jit(solution)/shard_map/ppermute | solution.py:292
  32.1 18.7 %collective-permute-start.12 = (f32[4,256,256]{2,1,0:T(8,128)}, f32[4,256,256]{2,1,0:T(8,128)S(1)}, u32[]{:S(2)}, u32[]{:S(2)}) collective-permute-start(f32[4,256,256]{2,1,0:T(8,128)} %get-tuple-element.18), channel_id=1, source_target_pairs={{8,0},{9,1},{10,2},{11,3},{12,4},{13,5},{14,6},{15,7}} | collective-permute-start | bytes 3145736 | tf_op jit(solution)/shard_map/ppermute | solution.py:286
  41.8 16.7 %collective-permute-start.4 = (f32[3,256,256]{2,1,0:T(8,128)S(1)}, f32[3,256,256]{2,1,0:T(8,128)}, u32[]{:S(2)}, u32[]{:S(2)}) collective-permute-start(f32[3,256,256]{2,1,0:T(8,128)S(1)} %collective-permute-done.3), channel_id=1, source_target_pairs={{0,2},{1,5},{8,10},{9,13},{16,18},{17,21},{24,26},{25,29}} | collective-permute-start | bytes 2359304 | tf_op jit(solution)/shard_map/ppermute | solution.py:307
  44.0 22.9 %collective-permute-start.27 = (f32[3,256,256]{2,1,0:T(8,128)S(1)}, f32[3,256,256]{2,1,0:T(8,128)}, u32[]{:S(2)}, u32[]{:S(2)}) collective-permute-start(f32[3,256,256]{2,1,0:T(8,128)S(1)} %collective-permute-done.26), channel_id=1, source_target_pairs={{0,2},{1,5},{8,10},{9,13},{16,18},{17,21},{24,26},{25,29}} | collective-permute-start | bytes 2359304 | tf_op jit(solution)/shard_map/ppermute | solution.py:307
  46.2 22.3 %collective-permute-start.1 = (f32[3,256,256]{2,1,0:T(8,128)S(1)}, f32[3,256,256]{2,1,0:T(8,128)}, u32[]{:S(2)}, u32[]{:S(2)}) collective-permute-start(f32[3,256,256]{2,1,0:T(8,128)S(1)} %collective-permute-done), channel_id=1, source_target_pairs={{2,6},{5,7},{10,14},{13,15},{18,22},{21,23},{26,30},{29,31}} | collective-permute-start | bytes 2359304 | tf_op jit(solution)/shard_map/ppermute | solution.py:307
  50.1 22.5 %collective-permute-start.20 = (f32[2,256,256]{2,1,0:T(8,128)S(1)}, f32[2,256,256]{2,1,0:T(8,128)S(1)}, u32[]{:S(2)}, u32[]{:S(2)}) collective-permute-start(f32[2,256,256]{2,1,0:T(8,128)S(1)} %copy-done.7), channel_id=1, source_target_pairs={{0,8},{8,16},{1,9},{9,17},{2,10},{10,18},{3,11},{11,19},{4,12},{12... | collective-permute-start | bytes 1572872 | tf_op jit(solution)/shard_map/ppermute | solution.py:292
  50.9 27.5 %collective-permute-start.24 = (f32[3,256,256]{2,1,0:T(8,128)}, f32[3,256,256]{2,1,0:T(8,128)}, u32[]{:S(2)}, u32[]{:S(2)}) collective-permute-start(f32[3,256,256]{2,1,0:T(8,128)} %collective-permute-done.23), channel_id=1, source_target_pairs={{2,6},{5,7},{10,14},{13,15},{18,22},{21,23},{26,30},{29,31}} | collective-permute-start | bytes 2359304 | tf_op jit(solution)/shard_map/ppermute | solution.py:307
  58.5 26.8 %collective-permute-start.5 = (f32[3,256,256]{2,1,0:T(8,128)}, f32[3,256,256]{2,1,0:T(8,128)}, u32[]{:S(2)}, u32[]{:S(2)}) collective-permute-start(f32[3,256,256]{2,1,0:T(8,128)} %collective-permute-done.4), channel_id=1, source_target_pairs={{2,6},{5,7},{10,14},{13,15},{18,22},{21,23},{26,30},{29,31}} | collective-permute-start | bytes 2359304 | tf_op jit(solution)/shard_map/ppermute | solution.py:307
  66.9 19.9 %collective-permute-start.28 = (f32[3,256,256]{2,1,0:T(8,128)}, f32[3,256,256]{2,1,0:T(8,128)}, u32[]{:S(2)}, u32[]{:S(2)}) collective-permute-start(f32[3,256,256]{2,1,0:T(8,128)} %collective-permute-done.27), channel_id=1, source_target_pairs={{2,6},{5,7},{10,14},{13,15},{18,22},{21,23},{26,30},{29,31}} | collective-permute-start | bytes 2359304 | tf_op jit(solution)/shard_map/ppermute | solution.py:307
  68.4 19.9 %collective-permute-start.2 = (f32[3,256,256]{2,1,0:T(8,128)}, f32[3,256,256]{2,1,0:T(8,128)}, u32[]{:S(2)}, u32[]{:S(2)}) collective-permute-start(f32[3,256,256]{2,1,0:T(8,128)} %collective-permute-done.1), channel_id=1, source_target_pairs={{6,4},{7,3},{14,12},{15,11},{22,20},{23,19},{30,28},{31,27}} | collective-permute-start | bytes 2359304 | tf_op jit(solution)/shard_map/ppermute | solution.py:307
  78.4 21.1 %collective-permute-start.25 = (f32[3,256,256]{2,1,0:T(8,128)}, f32[3,256,256]{2,1,0:T(8,128)}, u32[]{:S(2)}, u32[]{:S(2)}) collective-permute-start(f32[3,256,256]{2,1,0:T(8,128)} %collective-permute-done.24), channel_id=1, source_target_pairs={{6,4},{7,3},{14,12},{15,11},{22,20},{23,19},{30,28},{31,27}} | collective-permute-start | bytes 2359304 | tf_op jit(solution)/shard_map/ppermute | solution.py:307
  84.0 12.9 %collective-permute-start.21 = (f32[2,256,256]{2,1,0:T(8,128)S(1)}, f32[2,256,256]{2,1,0:T(8,128)S(1)}, u32[]{:S(2)}, u32[]{:S(2)}) collective-permute-start(f32[2,256,256]{2,1,0:T(8,128)S(1)} %collective-permute-done.20.refs_9_.refs_22_), channel_id=1, source_target_pairs={{8,16},{16,24},{9,17},{17,25},{10,18},{18,26},{11,19},{19,27},{12,... | collective-permute-start | bytes 1572872 | tf_op jit(solution)/shard_map/ppermute | solution.py:292
  86.8 14.9 %collective-permute-start.6 = (f32[3,256,256]{2,1,0:T(8,128)}, f32[3,256,256]{2,1,0:T(8,128)}, u32[]{:S(2)}, u32[]{:S(2)}) collective-permute-start(f32[3,256,256]{2,1,0:T(8,128)} %collective-permute-done.5), channel_id=1, source_target_pairs={{6,4},{7,3},{14,12},{15,11},{22,20},{23,19},{30,28},{31,27}} | collective-permute-start | bytes 2359304 | tf_op jit(solution)/shard_map/ppermute | solution.py:307
  88.4 18.0 %collective-permute-start.29 = (f32[3,256,256]{2,1,0:T(8,128)}, f32[3,256,256]{2,1,0:T(8,128)S(1)}, u32[]{:S(2)}, u32[]{:S(2)}) collective-permute-start(f32[3,256,256]{2,1,0:T(8,128)} %collective-permute-done.28), channel_id=1, source_target_pairs={{6,4},{7,3},{14,12},{15,11},{22,20},{23,19},{30,28},{31,27}} | collective-permute-start | bytes 2359304 | tf_op jit(solution)/shard_map/ppermute | solution.py:307
  98.3 16.6 %collective-permute-start.22 = (f32[2,256,256]{2,1,0:T(8,128)S(1)}, f32[2,256,256]{2,1,0:T(8,128)S(1)}, u32[]{:S(2)}, u32[]{:S(2)}) collective-permute-start(f32[2,256,256]{2,1,0:T(8,128)S(1)} %collective-permute-done.21.refs_10_.refs_23_), channel_id=1, source_target_pairs={{16,24},{17,25},{18,26},{19,27},{20,28},{21,29},{22,30},{23,31}} | collective-permute-start | bytes 1572872 | tf_op jit(solution)/shard_map/ppermute | solution.py:292
  101.6 39.4 %collective-permute-start.7 = (f32[3,256,256]{2,1,0:T(8,128)S(1)}, f32[3,256,256]{2,1,0:T(8,128)S(1)}, u32[]{:S(2)}, u32[]{:S(2)}) collective-permute-start(f32[3,256,256]{2,1,0:T(8,128)S(1)} %select_select_fusion.3.mine_a), channel_id=1, source_target_pairs={{0,1},{1,0},{2,3},{3,2},{4,5},{5,4},{6,7},{7,6},{8,9},{9,8},{10,11... | collective-permute-start | bytes 2359304 | tf_op jit(solution)/shard_map/ppermute | solution.py:311
  106.3 21.1 %collective-permute-start.30 = (f32[3,256,256]{2,1,0:T(8,128)S(1)}, f32[3,256,256]{2,1,0:T(8,128)S(1)}, u32[]{:S(2)}, u32[]{:S(2)}) collective-permute-start(f32[3,256,256]{2,1,0:T(8,128)S(1)} %select_select_fusion.1.mine_a), channel_id=1, source_target_pairs={{0,1},{1,0},{2,3},{3,2},{4,5},{5,4},{6,7},{7,6},{8,9},{9,8},{10,11... | collective-permute-start | bytes 2359304 | tf_op jit(solution)/shard_map/ppermute | solution.py:311
  107.8 33.2 %collective-permute-start.8 = (f32[3,256,256]{2,1,0:T(8,128)S(1)}, f32[3,256,256]{2,1,0:T(8,128)S(1)}, u32[]{:S(2)}, u32[]{:S(2)}) collective-permute-start(f32[3,256,256]{2,1,0:T(8,128)S(1)} %select_select_fusion.2.mine_b), channel_id=1, source_target_pairs={{0,1},{1,0},{2,3},{3,2},{4,5},{5,4},{6,7},{7,6},{8,9},{9,8},{10,11... | collective-permute-start | bytes 2359304 | tf_op jit(solution)/shard_map/ppermute | solution.py:311
  111.5 15.9 %collective-permute-start.31 = (f32[3,256,256]{2,1,0:T(8,128)S(1)}, f32[3,256,256]{2,1,0:T(8,128)S(1)}, u32[]{:S(2)}, u32[]{:S(2)}) collective-permute-start(f32[3,256,256]{2,1,0:T(8,128)S(1)} %select_select_fusion.mine_b), channel_id=1, source_target_pairs={{0,1},{1,0},{2,3},{3,2},{4,5},{5,4},{6,7},{7,6},{8,9},{9,8},{10,11... | collective-permute-start | bytes 2359304 | tf_op jit(solution)/shard_map/ppermute | solution.py:311
  (29 other events, 904.3 us)

commit v2 on v1

--- a/solution.py
+++ b/solution.py
@@ -90,76 +90,95 @@
         row_one[c] = one
         near = split(jnp.where(core == 0, g0, g1))
         far = split(jnp.where(core == 0, g1, g0))
-        for n, piece in enumerate((near[0], far[0], near[1], far[1], near[0], far[0])):
+        for n, piece in enumerate((near[0], near[1], near[0], far[0], far[1], far[0])):
             right[n * width:(n + 1) * width, cols] = piece
 
 
 def update_kernel(sizes, shift, place, pattern, values, mine_a, mine_b, other_a, other_b, right, one, *rest):
     nprow, npcol, half, count, base, ncols, width = sizes
-    out, blocks, sides, left, sems, side_sems, out_sems = rest[-7:]
+    out, blocks, sides, left, filled, sems, side_sems, out_sems = rest[-8:]
     prow, pcol, core = place[0], place[1], place[2]
-
-    def row0(part):
-        return jnp.where(part == 0, core, 1 - core) * half + base
+    total, ahead = 2 * count, 3
+
+    def row_of(n):
+        return jnp.where(n < count, core, 1 - core) * half + base + lax.rem(n, count)
 
     def fetch(n):
-        c, part = n // 2, n % 2
-        return pltpu.make_async_copy(values.at[pl.ds(row0(part), count), c], blocks.at[n], sems.at[n])
+        return pltpu.make_async_copy(values.at[row_of(n)], blocks.at[n], sems.at[n])
 
     def store(n):
-        c, part = n // 2, n % 2
-        return pltpu.make_async_copy(blocks.at[n], out.at[pl.ds(row0(part), count), c], out_sems.at[n])
-
-    def fetch_all(c):
-        fetch(2 * c).start()
-        fetch(2 * c + 1).start()
+        return pltpu.make_async_copy(blocks.at[n], out.at[row_of(n)], out_sems.at[n])
 
     sources = [pltpu.make_async_copy(ref, sides.at[n], side_sems.at[n]) for n, ref in enumerate((other_b, other_a))]
     for copy in sources:
         copy.start()
-    for c in range(min(2, ncols)):
-        fetch_all(c)
-    for part, (near, far) in enumerate(((mine_a, mine_b), (sides.at[0], sides.at[1]))):
+    for n in range(min(ahead, total)):
+        fetch(n).start()
+    for part, refs in enumerate(((mine_a, mine_b), (sides.at[0], sides.at[1]))):
         if part == 1:
             for copy in sources:
                 copy.wait()
-        near_high, near_low = split(near[...].reshape(count * width, width))
-        far_high, far_low = split(far[...].reshape(count * width, width))
-        rows = slice(part * count * width, (part + 1) * count * width)
-        for k, piece in enumerate((near_high, far_high, near_high, far_high, near_low, far_low)):
-            left[rows, k * width:(k + 1) * width] = piece
-    for c in range(ncols):
-        if c + 2 < ncols:
-            fetch_all(c + 2)
-        cols = slice(c * width, (c + 1) * width)
-        product = jnp.dot(left[...], right[:, cols], preferred_element_type=jnp.float32)
-        for part in range(2):
-            n = 2 * c + part
-            fetch(n).wait()
-            first = row0(part)
-            for r in range(count):
-                keep = pattern[first + r, c].astype(jnp.float32)
-                if c == 0:
-                    keep = jnp.where((pcol < 2) & ((first + r > 0) | (prow > 0)), 0.0, keep)
-                at = (part * count + r) * width
-                change = product[at:at + width]
-                if base == 0 and r == 0:
-                    change = jnp.where((first == 0) & (prow == 0), 0.0, change)
-                blocks[n, r] = blocks[n, r] * keep - change
-            for r in range(count):
-                row_g = (first + r) * nprow + prow
-
-                @pl.when((row_g == c * npcol + pcol) & (row_g != 1))
-                def _():
-                    blocks[n, r] = blocks[n, r] + shift * identity(width)
-
-            if base == 0:
-                @pl.when((first == 0) & (prow == 1))
-                def _():
-                    blocks[n, 0] = one[c]
-
-            store(n).start()
-    for n in range(2 * ncols):
+        for r in range(count):
+            n = part * count + r
+            for k, ref in enumerate(refs):
+                block = ref[r]
+                filled[n, k] = (jnp.max(jnp.abs(block)) > 0).astype(jnp.int32)
+                high, low = split(block)
+                for m, piece in enumerate((high, high, low)):
+                    left[n * width:(n + 1) * width, (3 * k + m) * width:(3 * k + m + 1) * width] = piece
+
+    def step(n, carry):
+        @pl.when(n + ahead < total)
+        def _():
+            fetch(n + ahead).start()
+
+        row = row_of(n)
+        row_g = row * nprow + prow
+        keep = [pattern[row, c].astype(jnp.float32) for c in range(ncols)]
+        keep[0] = jnp.where((pcol < 2) & (row_g > 0), 0.0, keep[0])
+        near, far = (filled[n, 0] > 0) & (row_g > 1), (filled[n, 1] > 0) & (row_g > 1)
+        rows = pl.ds(pl.multiple_of(n * width, width), width)
+        fetch(n).wait()
+
+        def run(inner):
+            for c in range(ncols):
+                product = jnp.dot(left[rows, inner], right[inner, c * width:(c + 1) * width], preferred_element_type=jnp.float32)
+                blocks[n, c] = blocks[n, c] * keep[c] - product
+
+        @pl.when(near & far)
+        def _():
+            run(slice(0, 6 * width))
+
+        @pl.when(near & jnp.logical_not(far))
+        def _():
+            run(slice(0, 3 * width))
+
+        @pl.when(far & jnp.logical_not(near))
+        def _():
+            run(slice(3 * width, 6 * width))
+
+        @pl.when(jnp.logical_not(near | far))
+        def _():
+            for c in range(ncols):
+                blocks[n, c] = blocks[n, c] * keep[c]
+
+        at = jnp.minimum(row_g // npcol, ncols - 1)
+
+        @pl.when((row_g == at * npcol + pcol) & ((row_g > 1) | (row_g == 0)))
+        def _():
+            blocks[n, at] = blocks[n, at] + shift * identity(width)
+
+        if base == 0:
+            @pl.when(row_g == 1)
+            def _():
+                for c in range(ncols):
+                    blocks[n, c] = one[c]
+
+        store(n).start()
+        return carry
+
+    lax.fori_loop(0, total, step, 0)
+    for n in range(total):
         store(n).wait()
 
 
@@ -167,12 +186,12 @@
     npcol, starts = sizes
     prow, pcol = place[0], place[1]
     ncols, width = values.shape[1], values.shape[2]
-    for c in range(ncols):
+    for c in range(1, ncols):
         on = jnp.where(c * npcol + pcol == prow, shift, 0.0)
         block = values[0, c] * pattern[0, c].astype(jnp.float32) + on * identity(width)
-        whole[c] = block
+        whole[c - 1] = block
         n = max(n for n in range(len(starts)) if starts[n] <= c)
-        parts[n][c - starts[n]] = block
+        parts[n - 1][c - starts[n]] = block
 
 
 def cols_kernel(sizes, shift, place, pattern, near, far, *parts):
@@ -261,14 +280,16 @@
     starts = [sum(counts[:n]) for n in range(len(counts))]
     rows = pl.pallas_call(
         functools.partial(rows_kernel, (npcol, tuple(starts)), shift),
-        out_shape=[array(ncols)] + [array(count) for count in counts],
+        out_shape=[array(ncols - 1)] + [array(count) for count in counts[1:]],
         grid_spec=pltpu.PrefetchScalarGridSpec(
             num_scalar_prefetch=2, grid=(1,),
             in_specs=[full(1, ncols)],
-            out_specs=[full(ncols)] + [full(count) for count in counts],
+            out_specs=[full(ncols - 1)] + [full(count) for count in counts[1:]],
         ),
         name="rows",
     )(place, pat, vals)
+    on = jnp.where(prow == pcol, shift, 0.0)
+    first_row = vals[0, 0:1] * pat[0, 0].astype(jnp.float32) + on * jnp.eye(width, dtype=jnp.float32)
     cols = pl.pallas_call(
         functools.partial(cols_kernel, (nprow, half, cut), shift),
         out_shape=[array(cut), array(half - cut)] * 2,
@@ -283,15 +304,16 @@
         name="cols",
     )(place, pat, vals, vals)
 
-    back = lax.ppermute(rows[0], "prow", [(1, 0)])
+    back0 = lax.ppermute(first_row, "prow", [(1, 0)])
+    back1 = lax.ppermute(rows[0], "prow", [(1, 0)])
     upper0, upper1 = [], []
     for n, (start, count) in enumerate(zip(starts, counts)):
-        hops = [rows[1 + n]]
+        hops = [rows[n] if n else first_row]
         for hop in range(1, nprow):
             pairs = [(hop - 1, hop)] + ([(hop, hop + 1)] if hop + 1 < nprow else [])
             hops.append(lax.ppermute(hops[-1], "prow", pairs))
         upper0.append((0, count, [(hop, 0) for hop in hops]))
-        upper1.append((0, count, [(back, start)] + [(hop, 0) for hop in hops[:-1]]))
+        upper1.append((0, count, [(back1, start - 1) if n else (back0, 0)] + [(hop, 0) for hop in hops[:-1]]))
     pivots = pick(place, [upper0[0], upper1[0]])
 
     swap_pairs = [(q, q ^ 1) for q in range(npcol)]
@@ -337,12 +359,13 @@
             in_specs=[smem, smem, anywhere, vmem, vmem, anywhere, anywhere, vmem, vmem] + [anywhere] * len(carried),
             out_specs=anywhere,
             scratch_shapes=[
-                pltpu.VMEM((2 * ncols, count, width, width), jnp.float32),
+                pltpu.VMEM((2 * count, ncols, width, width), jnp.float32),
                 pltpu.VMEM((2, count, width, width), jnp.float32),
                 pltpu.VMEM((2 * count * width, 6 * width), jnp.bfloat16),
-                pltpu.SemaphoreType.DMA((2 * ncols,)),
+                pltpu.SMEM((2 * count, 2), jnp.int32),
+                pltpu.SemaphoreType.DMA((2 * count,)),
                 pltpu.SemaphoreType.DMA((2,)),
-                pltpu.SemaphoreType.DMA((2 * ncols,)),
+                pltpu.SemaphoreType.DMA((2 * count,)),
             ],
             input_output_aliases={9: 0} if carried else {},
             compiler_params=pltpu.CompilerParams(vmem_limit_bytes=40 * 1024 * 1024),

time: 156 us -> 133 us (0.85)
  the two profiles are of different devices: /device:TPU:25 before, /device:TPU:6 now
where the time goes in v2:
time: 133 us; the launch traced here: 132 us
  starting transfers between devices  59.3 us (45%)
  Pallas kernels  32.4 us (24%)
  waiting for transfers between devices  28 us (21%)
  other arithmetic  8.12 us (6%)
  local copies, waits for them, and re-layouts  2.6 us (2%)
    ppermute x15, starting transfers between devices, body(): hops.append(lax.ppermute(hops[-1], 'pcol', pairs))  29.5 us
    ppermute x9, starting transfers between devices, body(): hops.append(lax.ppermute(hops[-1], 'prow', pairs))  25.5 us
    pallas_call x2, Pallas kernels, body(): pl.pallas_call(functools.partial(update_kernel, (nprow, npcol, half, coun...  15.2 us
    ppermute x15, waiting for transfers between devices, body(): hops.append(lax.ppermute(hops[-1], 'pcol', pairs))  9.8 us
    ppermute x1, waiting for transfers between devices, body(): back1 = lax.ppermute(rows[0], 'prow', [(1, 0)])  9.22 us
    pallas_call x1, Pallas kernels, body(): pl.pallas_call(functools.partial(factor_kernel, shift, plan), out_shape=[...  6.95 us
    select_n x5, other arithmetic, choose(): out = jnp.where(index == n, options[n], out)  6.48 us
    ppermute x9, waiting for transfers between devices, body(): hops.append(lax.ppermute(hops[-1], 'prow', pairs))  5.52 us
  transfers between devices with their start and end apart: 33, of which 8 were waited for; matrix products, arithmetic and copies ran while one was open for 7% of the time, Pallas kernels for 15%

profile of v2, /device:TPU:6, one launch (start us, length us, event | category | flops | bytes accessed | tf_op | source)
XLA Modules:
  0.0 131.6 jit_solution(17117180387420327045)
XLA Ops:
  2.0 4.4 %cols.1 = (f32[3,256,256]{2,1,0:T(8,128)}, f32[3,256,256]{2,1,0:T(8,128)}, f32[3,256,256]{2,1,0:T(8,128)}, f32[3,256,256]{2,1,0:T(8,128)}) custom-call(s32[4]{0:T(128)} %pad_add_fusion.place, s32[12,4]{1,0:T(8,128)} %copy.7.pattern, f32[12,4,256,256]{3,2,1,0:T(8,128)} %bitcast.14, f32[12,4,256,256]{3,2,1,0:T(8,128)} %bitcast.15), custom_call_target="tpu_custom_call" | custom-call | tf_op jit(solution)/shard_map/cols/pallas_call | solution.py:293
  11.1 1.6 %collective-permute-start = (f32[3,256,256]{2,1,0:T(8,128)}, f32[3,256,256]{2,1,0:T(8,128)}, u32[]{:S(2)}, u32[]{:S(2)}) collective-permute-start(f32[3,256,256]{2,1,0:T(8,128)} %get-tuple-element.14), channel_id=1, source_target_pairs={{0,2},{1,5},{8,10},{9,13},{16,18},{17,21},{24,26},{25,29}} | collective-permute-start | bytes 2359304 | tf_op jit(solution)/shard_map/ppermute | solution.py:329
  12.6 4.3 %collective-permute-start.9 = (f32[1,256,256]{2,1,0:T(8,128)S(1)}, f32[1,256,256]{2,1,0:T(8,128)S(1)}, u32[]{:S(2)}, u32[]{:S(2)}) collective-permute-start(f32[1,256,256]{2,1,0:T(8,128)S(1)} %fusion.1.refs_0_.refs_5_.refs_13_), channel_id=1, source_target_pairs={{0,8},{8,16},{1,9},{9,17},{2,10},{10,18},{3,11},{11,19},{4,12},{12... | collective-permute-start | bytes 786440 | tf_op jit(solution)/shard_map/ppermute | solution.py:314
  16.9 3.3 %rows.1 = (f32[3,256,256]{2,1,0:T(8,128)}, f32[1,256,256]{2,1,0:T(8,128)}, f32[2,256,256]{2,1,0:T(8,128)}) custom-call(s32[4]{0:T(128)} %pad_add_fusion.place, s32[12,4]{1,0:T(8,128)} %copy.7.pattern, f32[12,4,256,256]{3,2,1,0:T(8,128)} %bitcast.17), custom_call_target="tpu_custom_call" | custom-call | tf_op jit(solution)/shard_map/rows/pallas_call | solution.py:281
  20.3 2.2 %collective-permute-start.17 = (f32[1,256,256]{2,1,0:T(8,128)}, f32[1,256,256]{2,1,0:T(8,128)S(1)}, u32[]{:S(2)}, u32[]{:S(2)}) collective-permute-start(f32[1,256,256]{2,1,0:T(8,128)} %get-tuple-element.16.refs_4_.refs_17_), channel_id=1, source_target_pairs={{0,8},{8,16},{1,9},{9,17},{2,10},{10,18},{3,11},{11,19},{4,12},{12... | collective-permute-start | bytes 786440 | tf_op jit(solution)/shard_map/ppermute | solution.py:314
  24.5 4.2 %collective-permute-done.17.refs_5_.refs_18_ = f32[1,256,256]{2,1,0:T(8,128)S(1)} collective-permute-done((f32[1,256,256]{2,1,0:T(8,128)}, f32[1,256,256]{2,1,0:T(8,128)S(1)}, u32[]{:S(2)}, u32[]{:S(2)}) %collective-permute-start.17) | collective-permute-done | bytes 262176 | tf_op jit(solution)/shard_map/ppermute | solution.py:314
  36.4 14.8 %collective-permute-start.20 = (f32[2,256,256]{2,1,0:T(8,128)}, f32[2,256,256]{2,1,0:T(8,128)S(1)}, u32[]{:S(2)}, u32[]{:S(2)}) collective-permute-start(f32[2,256,256]{2,1,0:T(8,128)} %get-tuple-element.17.refs_8_.refs_21_), channel_id=1, source_target_pairs={{0,8},{8,16},{1,9},{9,17},{2,10},{10,18},{3,11},{11,19},{4,12},{12... | collective-permute-start | bytes 1572872 | tf_op jit(solution)/shard_map/ppermute | solution.py:314
  53.9 3.4 %collective-permute-start.2 = (f32[3,256,256]{2,1,0:T(8,128)}, f32[3,256,256]{2,1,0:T(8,128)}, u32[]{:S(2)}, u32[]{:S(2)}) collective-permute-start(f32[3,256,256]{2,1,0:T(8,128)} %collective-permute-done.1), channel_id=1, source_target_pairs={{6,4},{7,3},{14,12},{15,11},{22,20},{23,19},{30,28},{31,27}} | collective-permute-start | bytes 2359304 | tf_op jit(solution)/shard_map/ppermute | solution.py:329
  57.3 2.5 %pick.1 = f32[2,256,256]{2,1,0:T(8,128)} custom-call(s32[4]{0:T(128)} %pad_add_fusion.place, f32[1,256,256]{2,1,0:T(8,128)} %copy-done, f32[1,256,256]{2,1,0:T(8,128)} %copy-done.2, f32[1,256,256]{2,1,0:T(8,128)} %copy-done.4, f32[1,256,256]{2,1,0:T(8,128)} %copy-done.10, f32[1,256,256]{2,1,0:T(8,128)} %copy-done.8, f32[1,256,256]{2,1,0:T(8,128)} %copy-done, ...), custom_call_target="tpu_custom_call" | custom-call | tf_op jit(solution)/shard_map/pick/pallas_call | solution.py:239
  62.2 5.6 %collective-permute-start.26 = (f32[3,256,256]{2,1,0:T(8,128)}, f32[3,256,256]{2,1,0:T(8,128)}, u32[]{:S(2)}, u32[]{:S(2)}) collective-permute-start(f32[3,256,256]{2,1,0:T(8,128)} %collective-permute-done.25), channel_id=1, source_target_pairs={{6,4},{7,3},{14,12},{15,11},{22,20},{23,19},{30,28},{31,27}} | collective-permute-start | bytes 2359304 | tf_op jit(solution)/shard_map/ppermute | solution.py:329
  67.8 2.2 %collective-permute-start.6 = (f32[3,256,256]{2,1,0:T(8,128)}, f32[3,256,256]{2,1,0:T(8,128)}, u32[]{:S(2)}, u32[]{:S(2)}) collective-permute-start(f32[3,256,256]{2,1,0:T(8,128)} %collective-permute-done.5), channel_id=1, source_target_pairs={{6,4},{7,3},{14,12},{15,11},{22,20},{23,19},{30,28},{31,27}} | collective-permute-start | bytes 2359304 | tf_op jit(solution)/shard_map/ppermute | solution.py:329
  70.8 3.9 %collective-permute-done.29 = f32[3,256,256]{2,1,0:T(8,128)} collective-permute-done((f32[3,256,256]{2,1,0:T(8,128)}, f32[3,256,256]{2,1,0:T(8,128)}, u32[]{:S(2)}, u32[]{:S(2)}) %collective-permute-start.29) | collective-permute-done | bytes 786464 | tf_op jit(solution)/shard_map/ppermute | solution.py:329
  77.4 1.6 %select_select_fusion.3.mine_a = f32[3,256,256]{2,1,0:T(8,128)S(1)} fusion(f32[3,256,256]{2,1,0:T(8,128)} %collective-permute-done.2, f32[3,256,256]{2,1,0:T(8,128)} %collective-permute-done.1, f32[3,256,256]{2,1,0:T(8,128)} %collective-permute-done, f32[3,256,256]{2,1,0:T(8,128)} %get-tuple-element.14, pred[]{:T(512)S(6)} %eq.58, pred[]{:T(512)S(6)} %eq.57, ...), kind=kLoop, calls=%fused_computation.3 | loop fusion | flops 589824 | bytes 3932163 | tf_op jit(solution)/shard_map/jit(_where)/select_n | solution.py:256
  80.3 1.6 %select_select_fusion.1.mine_a = f32[3,256,256]{2,1,0:T(8,128)S(1)} fusion(f32[3,256,256]{2,1,0:T(8,128)} %collective-permute-done.26, f32[3,256,256]{2,1,0:T(8,128)} %collective-permute-done.25, f32[3,256,256]{2,1,0:T(8,128)} %collective-permute-done.24, f32[3,256,256]{2,1,0:T(8,128)} %get-tuple-element.21, pred[]{:T(512)S(6)} %eq.58, pred[]{:T(512)S(6)} %eq.57, ...), kind=kLoop, calls=%fused_computation.1 | loop fusion | flops 589824 | bytes 3932163 | tf_op jit(solution)/shard_map/jit(_where)/select_n | solution.py:256
  82.6 3.4 %collective-permute-done.14 = f32[2,256,256]{2,1,0:T(8,128)S(1)} collective-permute-done((f32[2,256,256]{2,1,0:T(8,128)}, f32[2,256,256]{2,1,0:T(8,128)S(1)}, u32[]{:S(2)}, u32[]{:S(2)}) %collective-permute-start.14) | collective-permute-done | bytes 524320 | tf_op jit(solution)/shard_map/ppermute | solution.py:329
  86.7 2.8 %collective-permute-start.15 = (f32[2,256,256]{2,1,0:T(8,128)S(1)}, f32[2,256,256]{2,1,0:T(8,128)S(1)}, u32[]{:S(2)}, u32[]{:S(2)}) collective-permute-start(f32[2,256,256]{2,1,0:T(8,128)S(1)} %collective-permute-done.14), channel_id=1, source_target_pairs={{6,4},{7,3},{14,12},{15,11},{22,20},{23,19},{30,28},{31,27}} | collective-permute-start | bytes 1572872 | tf_op jit(solution)/shard_map/ppermute | solution.py:329
  89.6 1.6 %select_select_fusion.2.mine_b = f32[3,256,256]{2,1,0:T(8,128)S(1)} fusion(f32[3,256,256]{2,1,0:T(8,128)} %collective-permute-done.6, f32[3,256,256]{2,1,0:T(8,128)} %collective-permute-done.5, f32[3,256,256]{2,1,0:T(8,128)} %collective-permute-done.4, f32[3,256,256]{2,1,0:T(8,128)} %collective-permute-done.3, pred[]{:T(512)S(6)} %eq.58, pred[]{:T(512)S(6)} %eq.57, ...), kind=kLoop, calls=%fused_computation.2 | loop fusion | flops 589824 | bytes 3932163 | tf_op jit(solution)/shard_map/jit(_where)/select_n | solution.py:256
  91.2 2.4 %collective-permute-done.30 = f32[3,256,256]{2,1,0:T(8,128)S(1)} collective-permute-done((f32[3,256,256]{2,1,0:T(8,128)}, f32[3,256,256]{2,1,0:T(8,128)S(1)}, u32[]{:S(2)}, u32[]{:S(2)}) %collective-permute-start.30) | collective-permute-done | bytes 786464 | tf_op jit(solution)/shard_map/ppermute | solution.py:329
  93.6 1.6 %select_select_fusion.mine_b = f32[3,256,256]{2,1,0:T(8,128)S(1)} fusion(f32[3,256,256]{2,1,0:T(8,128)S(1)} %collective-permute-done.30, f32[3,256,256]{2,1,0:T(8,128)} %collective-permute-done.29, f32[3,256,256]{2,1,0:T(8,128)} %collective-permute-done.28, f32[3,256,256]{2,1,0:T(8,128)} %collective-permute-done.27, pred[]{:T(512)S(6)} %eq.58, pred[]{:T(512)S(6)} %eq.57, ...), kind=kLoop, calls=%fused_computation | loop fusion | flops 589824 | bytes 3932163 | tf_op jit(solution)/shard_map/jit(_where)/select_n | solution.py:256
  95.7 9.2 %collective-permute-done.23.refs_16_.refs_20_ = f32[3,256,256]{2,1,0:T(8,128)S(1)} collective-permute-done((f32[3,256,256]{2,1,0:T(8,128)}, f32[3,256,256]{2,1,0:T(8,128)S(1)}, u32[]{:S(2)}, u32[]{:S(2)}) %collective-permute-start.23) | collective-permute-done | bytes 786464 | tf_op jit(solution)/shard_map/ppermute | solution.py:308
  105.7 3.4 %collective-permute-done.16.other_in = f32[2,256,256]{2,1,0:T(8,128)S(1)} collective-permute-done((f32[2,256,256]{2,1,0:T(8,128)S(1)}, f32[2,256,256]{2,1,0:T(8,128)S(1)}, u32[]{:S(2)}, u32[]{:S(2)}) %collective-permute-start.16) | collective-permute-done | bytes 524320 | tf_op jit(solution)/shard_map/ppermute | solution.py:333
  109.2 6.9 %factor.1 = (bf16[1536,1024]{1,0:T(8,128)(2,1)S(1)}, f32[4,256,256]{2,1,0:T(8,128)S(1)}) custom-call(s32[4]{0:T(128)S(1)} %copy-done.13, f32[2,256,256]{2,1,0:T(8,128)S(1)} %select_select_fusion.4.mine_in, f32[2,256,256]{2,1,0:T(8,128)S(1)} %collective-permute-done.16.other_in, f32[1,256,256]{2,1,0:T(8,128)S(1)} %copy-done.1, f32[1,256,256]{2,1,0:T(8,128)S(1)} %copy-done.3, ...), custom_call_target="tpu_custom_call" | custom-call | tf_op jit(solution)/shard_map/factor/pallas_call | solution.py:337
  116.2 7.6 %shard_map.28.rest_0_ = f32[12,4,256,256]{3,2,1,0:T(8,128)} custom-call(s32[4]{0:T(128)S(1)} %copy-done.13, s32[12,4]{1,0:T(8,128)S(1)} %copy-done.12, f32[12,4,256,256]{3,2,1,0:T(8,128)} %bitcast.18, f32[3,256,256]{2,1,0:T(8,128)S(1)} %select_select_fusion.1.mine_a, f32[3,256,256]{2,1,0:T(8,128)S(1)} %select_select_fusion.mine_b, ...), custom_call_target="tpu_custom_call" | custom-call | tf_op jit(solution)/shard_map/pallas_call | solution.py:356
  123.8 7.6 %shard_map.29 = f32[12,4,256,256]{3,2,1,0:T(8,128)} custom-call(s32[4]{0:T(128)S(1)} %copy-done.13, s32[12,4]{1,0:T(8,128)S(1)} %copy-done.12, f32[12,4,256,256]{3,2,1,0:T(8,128)} %bitcast.19, f32[3,256,256]{2,1,0:T(8,128)S(1)} %select_select_fusion.3.mine_a, f32[3,256,256]{2,1,0:T(8,128)S(1)} %select_select_fusion.2.mine_b, ...), custom_call_target="tpu_custom_call", output_to_operand_aliasing={{}: (9, {})} | custom-call | tf_op jit(solution)/shard_map/pallas_call | solution.py:356
  (87 shorter events, 28.2 us)
Async XLA Ops:
  6.4 22.9 %collective-permute-start.3 = (f32[3,256,256]{2,1,0:T(8,128)}, f32[3,256,256]{2,1,0:T(8,128)}, u32[]{:S(2)}, u32[]{:S(2)}) collective-permute-start(f32[3,256,256]{2,1,0:T(8,128)} %get-tuple-element.15), channel_id=1, source_target_pairs={{0,1},{1,0},{2,3},{3,2},{4,5},{5,4},{6,7},{7,6},{8,9},{9,8},{10,11... | collective-permute-start | bytes 2359304 | tf_op jit(solution)/shard_map/ppermute | solution.py:322
  10.5 21.1 %collective-permute-start.27 = (f32[3,256,256]{2,1,0:T(8,128)}, f32[3,256,256]{2,1,0:T(8,128)}, u32[]{:S(2)}, u32[]{:S(2)}) collective-permute-start(f32[3,256,256]{2,1,0:T(8,128)} %get-tuple-element.22), channel_id=1, source_target_pairs={{0,1},{1,0},{2,3},{3,2},{4,5},{5,4},{6,7},{7,6},{8,9},{9,8},{10,11... | collective-permute-start | bytes 2359304 | tf_op jit(solution)/shard_map/ppermute | solution.py:322
  11.1 22.1 %collective-permute-start = (f32[3,256,256]{2,1,0:T(8,128)}, f32[3,256,256]{2,1,0:T(8,128)}, u32[]{:S(2)}, u32[]{:S(2)}) collective-permute-start(f32[3,256,256]{2,1,0:T(8,128)} %get-tuple-element.14), channel_id=1, source_target_pairs={{0,2},{1,5},{8,10},{9,13},{16,18},{17,21},{24,26},{25,29}} | collective-permute-start | bytes 2359304 | tf_op jit(solution)/shard_map/ppermute | solution.py:329
  22.9 12.2 %collective-permute-start.24 = (f32[3,256,256]{2,1,0:T(8,128)}, f32[3,256,256]{2,1,0:T(8,128)}, u32[]{:S(2)}, u32[]{:S(2)}) collective-permute-start(f32[3,256,256]{2,1,0:T(8,128)} %get-tuple-element.21), channel_id=1, source_target_pairs={{0,2},{1,5},{8,10},{9,13},{16,18},{17,21},{24,26},{25,29}} | collective-permute-start | bytes 2359304 | tf_op jit(solution)/shard_map/ppermute | solution.py:329
  29.3 21.9 %collective-permute-start.4 = (f32[3,256,256]{2,1,0:T(8,128)}, f32[3,256,256]{2,1,0:T(8,128)}, u32[]{:S(2)}, u32[]{:S(2)}) collective-permute-start(f32[3,256,256]{2,1,0:T(8,128)} %collective-permute-done.3), channel_id=1, source_target_pairs={{0,2},{1,5},{8,10},{9,13},{16,18},{17,21},{24,26},{25,29}} | collective-permute-start | bytes 2359304 | tf_op jit(solution)/shard_map/ppermute | solution.py:329
  31.6 21.0 %collective-permute-start.28 = (f32[3,256,256]{2,1,0:T(8,128)}, f32[3,256,256]{2,1,0:T(8,128)}, u32[]{:S(2)}, u32[]{:S(2)}) collective-permute-start(f32[3,256,256]{2,1,0:T(8,128)} %collective-permute-done.27), channel_id=1, source_target_pairs={{0,2},{1,5},{8,10},{9,13},{16,18},{17,21},{24,26},{25,29}} | collective-permute-start | bytes 2359304 | tf_op jit(solution)/shard_map/ppermute | solution.py:329
  33.1 20.8 %collective-permute-start.1 = (f32[3,256,256]{2,1,0:T(8,128)}, f32[3,256,256]{2,1,0:T(8,128)}, u32[]{:S(2)}, u32[]{:S(2)}) collective-permute-start(f32[3,256,256]{2,1,0:T(8,128)} %collective-permute-done), channel_id=1, source_target_pairs={{2,6},{5,7},{10,14},{13,15},{18,22},{21,23},{26,30},{29,31}} | collective-permute-start | bytes 2359304 | tf_op jit(solution)/shard_map/ppermute | solution.py:329
  35.1 27.1 %collective-permute-start.25 = (f32[3,256,256]{2,1,0:T(8,128)}, f32[3,256,256]{2,1,0:T(8,128)}, u32[]{:S(2)}, u32[]{:S(2)}) collective-permute-start(f32[3,256,256]{2,1,0:T(8,128)} %collective-permute-done.24), channel_id=1, source_target_pairs={{2,6},{5,7},{10,14},{13,15},{18,22},{21,23},{26,30},{29,31}} | collective-permute-start | bytes 2359304 | tf_op jit(solution)/shard_map/ppermute | solution.py:329
  36.4 24.3 %collective-permute-start.20 = (f32[2,256,256]{2,1,0:T(8,128)}, f32[2,256,256]{2,1,0:T(8,128)S(1)}, u32[]{:S(2)}, u32[]{:S(2)}) collective-permute-start(f32[2,256,256]{2,1,0:T(8,128)} %get-tuple-element.17.refs_8_.refs_21_), channel_id=1, source_target_pairs={{0,8},{8,16},{1,9},{9,17},{2,10},{10,18},{3,11},{11,19},{4,12},{12... | collective-permute-start | bytes 1572872 | tf_op jit(solution)/shard_map/ppermute | solution.py:314
  51.3 16.5 %collective-permute-start.5 = (f32[3,256,256]{2,1,0:T(8,128)}, f32[3,256,256]{2,1,0:T(8,128)}, u32[]{:S(2)}, u32[]{:S(2)}) collective-permute-start(f32[3,256,256]{2,1,0:T(8,128)} %collective-permute-done.4), channel_id=1, source_target_pairs={{2,6},{5,7},{10,14},{13,15},{18,22},{21,23},{26,30},{29,31}} | collective-permute-start | bytes 2359304 | tf_op jit(solution)/shard_map/ppermute | solution.py:329
  52.6 22.2 %collective-permute-start.29 = (f32[3,256,256]{2,1,0:T(8,128)}, f32[3,256,256]{2,1,0:T(8,128)}, u32[]{:S(2)}, u32[]{:S(2)}) collective-permute-start(f32[3,256,256]{2,1,0:T(8,128)} %collective-permute-done.28), channel_id=1, source_target_pairs={{2,6},{5,7},{10,14},{13,15},{18,22},{21,23},{26,30},{29,31}} | collective-permute-start | bytes 2359304 | tf_op jit(solution)/shard_map/ppermute | solution.py:329
  53.9 22.2 %collective-permute-start.2 = (f32[3,256,256]{2,1,0:T(8,128)}, f32[3,256,256]{2,1,0:T(8,128)}, u32[]{:S(2)}, u32[]{:S(2)}) collective-permute-start(f32[3,256,256]{2,1,0:T(8,128)} %collective-permute-done.1), channel_id=1, source_target_pairs={{6,4},{7,3},{14,12},{15,11},{22,20},{23,19},{30,28},{31,27}} | collective-permute-start | bytes 2359304 | tf_op jit(solution)/shard_map/ppermute | solution.py:329
  62.2 16.8 %collective-permute-start.26 = (f32[3,256,256]{2,1,0:T(8,128)}, f32[3,256,256]{2,1,0:T(8,128)}, u32[]{:S(2)}, u32[]{:S(2)}) collective-permute-start(f32[3,256,256]{2,1,0:T(8,128)} %collective-permute-done.25), channel_id=1, source_target_pairs={{6,4},{7,3},{14,12},{15,11},{22,20},{23,19},{30,28},{31,27}} | collective-permute-start | bytes 2359304 | tf_op jit(solution)/shard_map/ppermute | solution.py:329
  67.8 18.9 %collective-permute-start.6 = (f32[3,256,256]{2,1,0:T(8,128)}, f32[3,256,256]{2,1,0:T(8,128)}, u32[]{:S(2)}, u32[]{:S(2)}) collective-permute-start(f32[3,256,256]{2,1,0:T(8,128)} %collective-permute-done.5), channel_id=1, source_target_pairs={{6,4},{7,3},{14,12},{15,11},{22,20},{23,19},{30,28},{31,27}} | collective-permute-start | bytes 2359304 | tf_op jit(solution)/shard_map/ppermute | solution.py:329
  70.0 11.9 %collective-permute-start.21 = (f32[2,256,256]{2,1,0:T(8,128)S(1)}, f32[2,256,256]{2,1,0:T(8,128)S(1)}, u32[]{:S(2)}, u32[]{:S(2)}) collective-permute-start(f32[2,256,256]{2,1,0:T(8,128)S(1)} %collective-permute-done.20.refs_9_.refs_22_), channel_id=1, source_target_pairs={{8,16},{16,24},{9,17},{17,25},{10,18},{18,26},{11,19},{19,27},{12,... | collective-permute-start | bytes 1572872 | tf_op jit(solution)/shard_map/ppermute | solution.py:314
  74.8 11.3 %collective-permute-start.14 = (f32[2,256,256]{2,1,0:T(8,128)}, f32[2,256,256]{2,1,0:T(8,128)S(1)}, u32[]{:S(2)}, u32[]{:S(2)}) collective-permute-start(f32[2,256,256]{2,1,0:T(8,128)} %collective-permute-done.13), channel_id=1, source_target_pairs={{2,6},{5,7},{10,14},{13,15},{18,22},{21,23},{26,30},{29,31}} | collective-permute-start | bytes 1572872 | tf_op jit(solution)/shard_map/ppermute | solution.py:329
  76.1 17.5 %collective-permute-start.30 = (f32[3,256,256]{2,1,0:T(8,128)}, f32[3,256,256]{2,1,0:T(8,128)S(1)}, u32[]{:S(2)}, u32[]{:S(2)}) collective-permute-start(f32[3,256,256]{2,1,0:T(8,128)} %collective-permute-done.29), channel_id=1, source_target_pairs={{6,4},{7,3},{14,12},{15,11},{22,20},{23,19},{30,28},{31,27}} | collective-permute-start | bytes 2359304 | tf_op jit(solution)/shard_map/ppermute | solution.py:329
  79.0 26.0 %collective-permute-start.23 = (f32[3,256,256]{2,1,0:T(8,128)}, f32[3,256,256]{2,1,0:T(8,128)S(1)}, u32[]{:S(2)}, u32[]{:S(2)}) collective-permute-start(f32[3,256,256]{2,1,0:T(8,128)} %get-tuple-element.18), channel_id=1, source_target_pairs={{8,0},{9,1},{10,2},{11,3},{12,4},{13,5},{14,6},{15,7}} | collective-permute-start | bytes 2359304 | tf_op jit(solution)/shard_map/ppermute | solution.py:308
  81.9 13.3 %collective-permute-start.19 = (f32[1,256,256]{2,1,0:T(8,128)S(1)}, f32[1,256,256]{2,1,0:T(8,128)S(1)}, u32[]{:S(2)}, u32[]{:S(2)}) collective-permute-start(f32[1,256,256]{2,1,0:T(8,128)S(1)} %collective-permute-done.18.refs_6_.refs_19_), channel_id=1, source_target_pairs={{16,24},{17,25},{18,26},{19,27},{20,28},{21,29},{22,30},{23,31}} | collective-permute-start | bytes 786440 | tf_op jit(solution)/shard_map/ppermute | solution.py:314
  86.0 19.6 %collective-permute-start.22 = (f32[2,256,256]{2,1,0:T(8,128)S(1)}, f32[2,256,256]{2,1,0:T(8,128)S(1)}, u32[]{:S(2)}, u32[]{:S(2)}) collective-permute-start(f32[2,256,256]{2,1,0:T(8,128)S(1)} %collective-permute-done.21.refs_10_.refs_23_), channel_id=1, source_target_pairs={{16,24},{17,25},{18,26},{19,27},{20,28},{21,29},{22,30},{23,31}} | collective-permute-start | bytes 1572872 | tf_op jit(solution)/shard_map/ppermute | solution.py:314
  86.7 18.2 %collective-permute-start.15 = (f32[2,256,256]{2,1,0:T(8,128)S(1)}, f32[2,256,256]{2,1,0:T(8,128)S(1)}, u32[]{:S(2)}, u32[]{:S(2)}) collective-permute-start(f32[2,256,256]{2,1,0:T(8,128)S(1)} %collective-permute-done.14), channel_id=1, source_target_pairs={{6,4},{7,3},{14,12},{15,11},{22,20},{23,19},{30,28},{31,27}} | collective-permute-start | bytes 1572872 | tf_op jit(solution)/shard_map/ppermute | solution.py:329
  93.6 30.2 %collective-permute-start.7 = (f32[3,256,256]{2,1,0:T(8,128)S(1)}, f32[3,256,256]{2,1,0:T(8,128)S(1)}, u32[]{:S(2)}, u32[]{:S(2)}) collective-permute-start(f32[3,256,256]{2,1,0:T(8,128)S(1)} %select_select_fusion.3.mine_a), channel_id=1, source_target_pairs={{0,1},{1,0},{2,3},{3,2},{4,5},{5,4},{6,7},{7,6},{8,9},{9,8},{10,11... | collective-permute-start | bytes 2359304 | tf_op jit(solution)/shard_map/ppermute | solution.py:333
  95.2 21.0 %collective-permute-start.31 = (f32[3,256,256]{2,1,0:T(8,128)S(1)}, f32[3,256,256]{2,1,0:T(8,128)S(1)}, u32[]{:S(2)}, u32[]{:S(2)}) collective-permute-start(f32[3,256,256]{2,1,0:T(8,128)S(1)} %select_select_fusion.1.mine_a), channel_id=1, source_target_pairs={{0,1},{1,0},{2,3},{3,2},{4,5},{5,4},{6,7},{7,6},{8,9},{9,8},{10,11... | collective-permute-start | bytes 2359304 | tf_op jit(solution)/shard_map/ppermute | solution.py:333
  105.0 18.8 %collective-permute-start.8 = (f32[3,256,256]{2,1,0:T(8,128)S(1)}, f32[3,256,256]{2,1,0:T(8,128)S(1)}, u32[]{:S(2)}, u32[]{:S(2)}) collective-permute-start(f32[3,256,256]{2,1,0:T(8,128)S(1)} %select_select_fusion.2.mine_b), channel_id=1, source_target_pairs={{0,1},{1,0},{2,3},{3,2},{4,5},{5,4},{6,7},{7,6},{8,9},{9,8},{10,11... | collective-permute-start | bytes 2359304 | tf_op jit(solution)/shard_map/ppermute | solution.py:333
  (24 other events, 814.2 us)

commit v3 on v2

--- a/solution.py
+++ b/solution.py
@@ -182,16 +182,12 @@
         store(n).wait()
 
 
-def rows_kernel(sizes, shift, place, pattern, values, whole, *parts):
-    npcol, starts = sizes
+def rows_kernel(npcol, shift, place, pattern, values, out):
     prow, pcol = place[0], place[1]
     ncols, width = values.shape[1], values.shape[2]
     for c in range(1, ncols):
         on = jnp.where(c * npcol + pcol == prow, shift, 0.0)
-        block = values[0, c] * pattern[0, c].astype(jnp.float32) + on * identity(width)
-        whole[c - 1] = block
-        n = max(n for n in range(len(starts)) if starts[n] <= c)
-        parts[n - 1][c - starts[n]] = block
+        out[c - 1] = values[0, c] * pattern[0, c].astype(jnp.float32) + on * identity(width)
 
 
 def cols_kernel(sizes, shift, place, pattern, near, far, *parts):
@@ -276,15 +272,15 @@
     array = lambda *shape: jax.ShapeDtypeStruct(shape + (width, width), jnp.float32)
     full = lambda *shape: pl.BlockSpec(shape + (width, width), lambda *_: (0,) * (len(shape) + 2))
 
-    counts = [1, 1, ncols - 2] if ncols > 2 else [1] * ncols
+    counts = [1, ncols - 1]
     starts = [sum(counts[:n]) for n in range(len(counts))]
     rows = pl.pallas_call(
-        functools.partial(rows_kernel, (npcol, tuple(starts)), shift),
-        out_shape=[array(ncols - 1)] + [array(count) for count in counts[1:]],
+        functools.partial(rows_kernel, npcol, shift),
+        out_shape=[array(ncols - 1)],
         grid_spec=pltpu.PrefetchScalarGridSpec(
             num_scalar_prefetch=2, grid=(1,),
             in_specs=[full(1, ncols)],
-            out_specs=[full(ncols - 1)] + [full(count) for count in counts[1:]],
+            out_specs=[full(ncols - 1)],
         ),
         name="rows",
     )(place, pat, vals)
@@ -308,7 +304,7 @@
     back1 = lax.ppermute(rows[0], "prow", [(1, 0)])
     upper0, upper1 = [], []
     for n, (start, count) in enumerate(zip(starts, counts)):
-        hops = [rows[n] if n else first_row]
+        hops = [rows[0] if n else first_row]
         for hop in range(1, nprow):
             pairs = [(hop - 1, hop)] + ([(hop, hop + 1)] if hop + 1 < nprow else [])
             hops.append(lax.ppermute(hops[-1], "prow", pairs))

time: 133 us -> 129 us (0.970)
  the two profiles are of different devices: /device:TPU:6 before, /device:TPU:13 now
where the time goes in v3:
time: 129 us; the launch traced here: 128 us
  starting transfers between devices  69.5 us (54%)
  Pallas kernels  30.2 us (23%)
  waiting for transfers between devices  16.3 us (13%)
  other arithmetic  8.29 us (6%)
  local copies, waits for them, and re-layouts  2.66 us (2%)
  between operations  1.33 us (1%)
    ppermute x15, starting transfers between devices, body(): hops.append(lax.ppermute(hops[-1], 'pcol', pairs))  31.8 us
    ppermute x5, starting transfers between devices, body(): swapped.append(lax.ppermute(chunk, 'pcol', swap_pairs))  19.8 us
    ppermute x6, starting transfers between devices, body(): hops.append(lax.ppermute(hops[-1], 'prow', pairs))  14.1 us
    pallas_call x2, Pallas kernels, body(): pl.pallas_call(functools.partial(update_kernel, (nprow, npcol, half, coun...  13.4 us
    ppermute x15, waiting for transfers between devices, body(): hops.append(lax.ppermute(hops[-1], 'pcol', pairs))  7.31 us
    pallas_call x1, Pallas kernels, body(): pl.pallas_call(functools.partial(factor_kernel, shift, plan), out_shape=[...  6.82 us
    select_n x5, other arithmetic, choose(): out = jnp.where(index == n, options[n], out)  6.68 us
    ppermute x6, waiting for transfers between devices, body(): hops.append(lax.ppermute(hops[-1], 'prow', pairs))  6.44 us
  transfers between devices with their start and end apart: 30, of which 8 were waited for; matrix products, arithmetic and copies ran while one was open for 7% of the time, Pallas kernels for 18%

profile of v3, /device:TPU:13, one launch (start us, length us, event | category | flops | bytes accessed | tf_op | source)
XLA Modules:
  0.0 128.2 jit_solution(4773915252035122438)
XLA Ops:
  2.9 3.2 %collective-permute-start.9 = (f32[1,256,256]{2,1,0:T(8,128)S(1)}, f32[1,256,256]{2,1,0:T(8,128)S(1)}, u32[]{:S(2)}, u32[]{:S(2)}) collective-permute-start(f32[1,256,256]{2,1,0:T(8,128)S(1)} %fusion.1.refs_0_.refs_5_.refs_9_), channel_id=1, source_target_pairs={{0,8},{8,16},{1,9},{9,17},{2,10},{10,18},{3,11},{11,19},{4,12},{12... | collective-permute-start | bytes 786440 | tf_op jit(solution)/shard_map/ppermute | solution.py:310
  8.2 4.4 %cols.1 = (f32[3,256,256]{2,1,0:T(8,128)}, f32[3,256,256]{2,1,0:T(8,128)}, f32[3,256,256]{2,1,0:T(8,128)}, f32[3,256,256]{2,1,0:T(8,128)}) custom-call(s32[4]{0:T(128)} %pad_add_fusion.place, s32[12,4]{1,0:T(8,128)} %copy.7.pattern, f32[12,4,256,256]{3,2,1,0:T(8,128)} %bitcast.15, f32[12,4,256,256]{3,2,1,0:T(8,128)} %bitcast.16), custom_call_target="tpu_custom_call" | custom-call | tf_op jit(solution)/shard_map/cols/pallas_call | solution.py:289
  17.6 3.5 %collective-permute-done.10.refs_2_.refs_7_.refs_11_ = f32[1,256,256]{2,1,0:T(8,128)S(1)} collective-permute-done((f32[1,256,256]{2,1,0:T(8,128)S(1)}, f32[1,256,256]{2,1,0:T(8,128)S(1)}, u32[]{:S(2)}, u32[]{:S(2)}) %collective-permute-start.10) | collective-permute-done | bytes 262176 | tf_op jit(solution)/shard_map/ppermute | solution.py:310
  23.8 3.0 %rows.1.refs_4_.refs_13_ = f32[3,256,256]{2,1,0:T(8,128)} custom-call(s32[4]{0:T(128)} %pad_add_fusion.place, s32[12,4]{1,0:T(8,128)} %copy.7.pattern, f32[12,4,256,256]{3,2,1,0:T(8,128)} %bitcast.17), custom_call_target="tpu_custom_call" | custom-call | tf_op jit(solution)/shard_map/rows/pallas_call | solution.py:277
  26.8 5.1 %collective-permute-start.17 = (f32[3,256,256]{2,1,0:T(8,128)}, f32[3,256,256]{2,1,0:T(8,128)S(1)}, u32[]{:S(2)}, u32[]{:S(2)}) collective-permute-start(f32[3,256,256]{2,1,0:T(8,128)} %rows.1.refs_4_.refs_13_), channel_id=1, source_target_pairs={{0,8},{8,16},{1,9},{9,17},{2,10},{10,18},{3,11},{11,19},{4,12},{12... | collective-permute-start | bytes 2359304 | tf_op jit(solution)/shard_map/ppermute | solution.py:310
  34.5 5.3 %collective-permute-start.1 = (f32[3,256,256]{2,1,0:T(8,128)}, f32[3,256,256]{2,1,0:T(8,128)}, u32[]{:S(2)}, u32[]{:S(2)}) collective-permute-start(f32[3,256,256]{2,1,0:T(8,128)} %collective-permute-done), channel_id=1, source_target_pairs={{2,6},{5,7},{10,14},{13,15},{18,22},{21,23},{26,30},{29,31}} | collective-permute-start | bytes 2359304 | tf_op jit(solution)/shard_map/ppermute | solution.py:325
  39.8 2.2 %collective-permute-start.22 = (f32[3,256,256]{2,1,0:T(8,128)}, f32[3,256,256]{2,1,0:T(8,128)}, u32[]{:S(2)}, u32[]{:S(2)}) collective-permute-start(f32[3,256,256]{2,1,0:T(8,128)} %collective-permute-done.21), channel_id=1, source_target_pairs={{2,6},{5,7},{10,14},{13,15},{18,22},{21,23},{26,30},{29,31}} | collective-permute-start | bytes 2359304 | tf_op jit(solution)/shard_map/ppermute | solution.py:325
  42.0 2.5 %pick.1 = f32[2,256,256]{2,1,0:T(8,128)} custom-call(s32[4]{0:T(128)} %pad_add_fusion.place, f32[1,256,256]{2,1,0:T(8,128)} %copy-done.1, f32[1,256,256]{2,1,0:T(8,128)} %copy-done.3, f32[1,256,256]{2,1,0:T(8,128)} %copy-done.5, f32[1,256,256]{2,1,0:T(8,128)} %copy-done.9, f32[1,256,256]{2,1,0:T(8,128)} %copy-done.7, f32[1,256,256]{2,1,0:T(8,128)} %copy-done.1, ...), custom_call_target="tpu_custom_call" | custom-call | tf_op jit(solution)/shard_map/pick/pallas_call | solution.py:235
  44.5 2.4 %collective-permute-done.17.refs_5_.refs_14_ = f32[3,256,256]{2,1,0:T(8,128)S(1)} collective-permute-done((f32[3,256,256]{2,1,0:T(8,128)}, f32[3,256,256]{2,1,0:T(8,128)S(1)}, u32[]{:S(2)}, u32[]{:S(2)}) %collective-permute-start.17) | collective-permute-done | bytes 786464 | tf_op jit(solution)/shard_map/ppermute | solution.py:310
  48.2 5.3 %collective-permute-start.5 = (f32[3,256,256]{2,1,0:T(8,128)}, f32[3,256,256]{2,1,0:T(8,128)}, u32[]{:S(2)}, u32[]{:S(2)}) collective-permute-start(f32[3,256,256]{2,1,0:T(8,128)} %collective-permute-done.4), channel_id=1, source_target_pairs={{2,6},{5,7},{10,14},{13,15},{18,22},{21,23},{26,30},{29,31}} | collective-permute-start | bytes 2359304 | tf_op jit(solution)/shard_map/ppermute | solution.py:325
  53.5 1.7 %collective-permute-done.25 = f32[3,256,256]{2,1,0:T(8,128)} collective-permute-done((f32[3,256,256]{2,1,0:T(8,128)}, f32[3,256,256]{2,1,0:T(8,128)}, u32[]{:S(2)}, u32[]{:S(2)}) %collective-permute-start.25) | collective-permute-done | bytes 786464 | tf_op jit(solution)/shard_map/ppermute | solution.py:325
  55.2 2.2 %collective-permute-start.26 = (f32[3,256,256]{2,1,0:T(8,128)}, f32[3,256,256]{2,1,0:T(8,128)}, u32[]{:S(2)}, u32[]{:S(2)}) collective-permute-start(f32[3,256,256]{2,1,0:T(8,128)} %collective-permute-done.25), channel_id=1, source_target_pairs={{2,6},{5,7},{10,14},{13,15},{18,22},{21,23},{26,30},{29,31}} | collective-permute-start | bytes 2359304 | tf_op jit(solution)/shard_map/ppermute | solution.py:325
  57.4 1.6 %collective-permute-start.2 = (f32[3,256,256]{2,1,0:T(8,128)}, f32[3,256,256]{2,1,0:T(8,128)}, u32[]{:S(2)}, u32[]{:S(2)}) collective-permute-start(f32[3,256,256]{2,1,0:T(8,128)} %collective-permute-done.1), channel_id=1, source_target_pairs={{6,4},{7,3},{14,12},{15,11},{22,20},{23,19},{30,28},{31,27}} | collective-permute-start | bytes 2359304 | tf_op jit(solution)/shard_map/ppermute | solution.py:325
  59.0 2.1 %collective-permute-done.13 = f32[2,256,256]{2,1,0:T(8,128)} collective-permute-done((f32[2,256,256]{2,1,0:T(8,128)}, f32[2,256,256]{2,1,0:T(8,128)}, u32[]{:S(2)}, u32[]{:S(2)}) %collective-permute-start.13) | collective-permute-done | bytes 524320 | tf_op jit(solution)/shard_map/ppermute | solution.py:325
  61.1 3.1 %collective-permute-start.18 = (f32[3,256,256]{2,1,0:T(8,128)S(1)}, f32[3,256,256]{2,1,0:T(8,128)S(1)}, u32[]{:S(2)}, u32[]{:S(2)}) collective-permute-start(f32[3,256,256]{2,1,0:T(8,128)S(1)} %collective-permute-done.17.refs_5_.refs_14_), channel_id=1, source_target_pairs={{8,16},{16,24},{9,17},{17,25},{10,18},{18,26},{11,19},{19,27},{12,... | collective-permute-start | bytes 2359304 | tf_op jit(solution)/shard_map/ppermute | solution.py:310
  65.8 4.1 %collective-permute-start.14 = (f32[2,256,256]{2,1,0:T(8,128)}, f32[2,256,256]{2,1,0:T(8,128)}, u32[]{:S(2)}, u32[]{:S(2)}) collective-permute-start(f32[2,256,256]{2,1,0:T(8,128)} %collective-permute-done.13), channel_id=1, source_target_pairs={{2,6},{5,7},{10,14},{13,15},{18,22},{21,23},{26,30},{29,31}} | collective-permute-start | bytes 1572872 | tf_op jit(solution)/shard_map/ppermute | solution.py:325
  69.9 3.5 %collective-permute-done.26 = f32[3,256,256]{2,1,0:T(8,128)} collective-permute-done((f32[3,256,256]{2,1,0:T(8,128)}, f32[3,256,256]{2,1,0:T(8,128)}, u32[]{:S(2)}, u32[]{:S(2)}) %collective-permute-start.26) | collective-permute-done | bytes 786464 | tf_op jit(solution)/shard_map/ppermute | solution.py:325
  81.9 8.6 %collective-permute-start.7 = (f32[3,256,256]{2,1,0:T(8,128)S(1)}, f32[3,256,256]{2,1,0:T(8,128)S(1)}, u32[]{:S(2)}, u32[]{:S(2)}) collective-permute-start(f32[3,256,256]{2,1,0:T(8,128)S(1)} %select_select_fusion.3.mine_a), channel_id=1, source_target_pairs={{0,1},{1,0},{2,3},{3,2},{4,5},{5,4},{6,7},{7,6},{8,9},{9,8},{10,11... | collective-permute-start | bytes 2359304 | tf_op jit(solution)/shard_map/ppermute | solution.py:329
  91.8 7.0 %collective-permute-start.28 = (f32[3,256,256]{2,1,0:T(8,128)S(1)}, f32[3,256,256]{2,1,0:T(8,128)S(1)}, u32[]{:S(2)}, u32[]{:S(2)}) collective-permute-start(f32[3,256,256]{2,1,0:T(8,128)S(1)} %select_select_fusion.1.mine_a), channel_id=1, source_target_pairs={{0,1},{1,0},{2,3},{3,2},{4,5},{5,4},{6,7},{7,6},{8,9},{9,8},{10,11... | collective-permute-start | bytes 2359304 | tf_op jit(solution)/shard_map/ppermute | solution.py:329
  100.3 4.1 %collective-permute-start.29 = (f32[3,256,256]{2,1,0:T(8,128)S(1)}, f32[3,256,256]{2,1,0:T(8,128)S(1)}, u32[]{:S(2)}, u32[]{:S(2)}) collective-permute-start(f32[3,256,256]{2,1,0:T(8,128)S(1)} %select_select_fusion.mine_b), channel_id=1, source_target_pairs={{0,1},{1,0},{2,3},{3,2},{4,5},{5,4},{6,7},{7,6},{8,9},{9,8},{10,11... | collective-permute-start | bytes 2359304 | tf_op jit(solution)/shard_map/ppermute | solution.py:329
  105.8 1.9 %collective-permute-done.16.other_in = f32[2,256,256]{2,1,0:T(8,128)S(1)} collective-permute-done((f32[2,256,256]{2,1,0:T(8,128)S(1)}, f32[2,256,256]{2,1,0:T(8,128)S(1)}, u32[]{:S(2)}, u32[]{:S(2)}) %collective-permute-start.16) | collective-permute-done | bytes 524320 | tf_op jit(solution)/shard_map/ppermute | solution.py:329
  107.7 6.8 %factor.1 = (bf16[1536,1024]{1,0:T(8,128)(2,1)S(1)}, f32[4,256,256]{2,1,0:T(8,128)S(1)}) custom-call(s32[4]{0:T(128)S(1)} %copy-done.12, f32[2,256,256]{2,1,0:T(8,128)S(1)} %select_select_fusion.4.mine_in, f32[2,256,256]{2,1,0:T(8,128)S(1)} %collective-permute-done.16.other_in, f32[1,256,256]{2,1,0:T(8,128)S(1)} %copy-done.2, f32[1,256,256]{2,1,0:T(8,128)S(1)} %copy-done.4, ...), custom_call_target="tpu_custom_call" | custom-call | tf_op jit(solution)/shard_map/factor/pallas_call | solution.py:333
  114.6 6.6 %shard_map.28.rest_0_ = f32[12,4,256,256]{3,2,1,0:T(8,128)} custom-call(s32[4]{0:T(128)S(1)} %copy-done.12, s32[12,4]{1,0:T(8,128)S(1)} %copy-done.11, f32[12,4,256,256]{3,2,1,0:T(8,128)} %bitcast.18, f32[3,256,256]{2,1,0:T(8,128)S(1)} %select_select_fusion.1.mine_a, f32[3,256,256]{2,1,0:T(8,128)S(1)} %select_select_fusion.mine_b, ...), custom_call_target="tpu_custom_call" | custom-call | tf_op jit(solution)/shard_map/pallas_call | solution.py:352
  121.2 6.8 %shard_map.29 = f32[12,4,256,256]{3,2,1,0:T(8,128)} custom-call(s32[4]{0:T(128)S(1)} %copy-done.12, s32[12,4]{1,0:T(8,128)S(1)} %copy-done.11, f32[12,4,256,256]{3,2,1,0:T(8,128)} %bitcast.19, f32[3,256,256]{2,1,0:T(8,128)S(1)} %select_select_fusion.3.mine_a, f32[3,256,256]{2,1,0:T(8,128)S(1)} %select_select_fusion.2.mine_b, ...), custom_call_target="tpu_custom_call", output_to_operand_aliasing={{}: (9, {})} | custom-call | tf_op jit(solution)/shard_map/pallas_call | solution.py:352
  (79 shorter events, 29.9 us)
Async XLA Ops:
  12.6 19.3 %collective-permute-start.3 = (f32[3,256,256]{2,1,0:T(8,128)}, f32[3,256,256]{2,1,0:T(8,128)}, u32[]{:S(2)}, u32[]{:S(2)}) collective-permute-start(f32[3,256,256]{2,1,0:T(8,128)} %get-tuple-element.12), channel_id=1, source_target_pairs={{0,1},{1,0},{2,3},{3,2},{4,5},{5,4},{6,7},{7,6},{8,9},{9,8},{10,11... | collective-permute-start | bytes 2359304 | tf_op jit(solution)/shard_map/ppermute | solution.py:318
  13.5 19.7 %collective-permute-start.24 = (f32[3,256,256]{2,1,0:T(8,128)}, f32[3,256,256]{2,1,0:T(8,128)}, u32[]{:S(2)}, u32[]{:S(2)}) collective-permute-start(f32[3,256,256]{2,1,0:T(8,128)} %get-tuple-element.16), channel_id=1, source_target_pairs={{0,1},{1,0},{2,3},{3,2},{4,5},{5,4},{6,7},{7,6},{8,9},{9,8},{10,11... | collective-permute-start | bytes 2359304 | tf_op jit(solution)/shard_map/ppermute | solution.py:318
  13.5 21.0 %collective-permute-start = (f32[3,256,256]{2,1,0:T(8,128)}, f32[3,256,256]{2,1,0:T(8,128)}, u32[]{:S(2)}, u32[]{:S(2)}) collective-permute-start(f32[3,256,256]{2,1,0:T(8,128)} %get-tuple-element.11), channel_id=1, source_target_pairs={{0,2},{1,5},{8,10},{9,13},{16,18},{17,21},{24,26},{25,29}} | collective-permute-start | bytes 2359304 | tf_op jit(solution)/shard_map/ppermute | solution.py:325
  22.5 17.3 %collective-permute-start.21 = (f32[3,256,256]{2,1,0:T(8,128)}, f32[3,256,256]{2,1,0:T(8,128)}, u32[]{:S(2)}, u32[]{:S(2)}) collective-permute-start(f32[3,256,256]{2,1,0:T(8,128)} %get-tuple-element.15), channel_id=1, source_target_pairs={{0,2},{1,5},{8,10},{9,13},{16,18},{17,21},{24,26},{25,29}} | collective-permute-start | bytes 2359304 | tf_op jit(solution)/shard_map/ppermute | solution.py:325
  26.8 20.1 %collective-permute-start.17 = (f32[3,256,256]{2,1,0:T(8,128)}, f32[3,256,256]{2,1,0:T(8,128)S(1)}, u32[]{:S(2)}, u32[]{:S(2)}) collective-permute-start(f32[3,256,256]{2,1,0:T(8,128)} %rows.1.refs_4_.refs_13_), channel_id=1, source_target_pairs={{0,8},{8,16},{1,9},{9,17},{2,10},{10,18},{3,11},{11,19},{4,12},{12... | collective-permute-start | bytes 2359304 | tf_op jit(solution)/shard_map/ppermute | solution.py:310
  31.9 16.3 %collective-permute-start.4 = (f32[3,256,256]{2,1,0:T(8,128)}, f32[3,256,256]{2,1,0:T(8,128)}, u32[]{:S(2)}, u32[]{:S(2)}) collective-permute-start(f32[3,256,256]{2,1,0:T(8,128)} %collective-permute-done.3), channel_id=1, source_target_pairs={{0,2},{1,5},{8,10},{9,13},{16,18},{17,21},{24,26},{25,29}} | collective-permute-start | bytes 2359304 | tf_op jit(solution)/shard_map/ppermute | solution.py:325
  33.2 22.0 %collective-permute-start.25 = (f32[3,256,256]{2,1,0:T(8,128)}, f32[3,256,256]{2,1,0:T(8,128)}, u32[]{:S(2)}, u32[]{:S(2)}) collective-permute-start(f32[3,256,256]{2,1,0:T(8,128)} %collective-permute-done.24), channel_id=1, source_target_pairs={{0,2},{1,5},{8,10},{9,13},{16,18},{17,21},{24,26},{25,29}} | collective-permute-start | bytes 2359304 | tf_op jit(solution)/shard_map/ppermute | solution.py:325
  34.5 22.9 %collective-permute-start.1 = (f32[3,256,256]{2,1,0:T(8,128)}, f32[3,256,256]{2,1,0:T(8,128)}, u32[]{:S(2)}, u32[]{:S(2)}) collective-permute-start(f32[3,256,256]{2,1,0:T(8,128)} %collective-permute-done), channel_id=1, source_target_pairs={{2,6},{5,7},{10,14},{13,15},{18,22},{21,23},{26,30},{29,31}} | collective-permute-start | bytes 2359304 | tf_op jit(solution)/shard_map/ppermute | solution.py:325
  39.8 24.4 %collective-permute-start.22 = (f32[3,256,256]{2,1,0:T(8,128)}, f32[3,256,256]{2,1,0:T(8,128)}, u32[]{:S(2)}, u32[]{:S(2)}) collective-permute-start(f32[3,256,256]{2,1,0:T(8,128)} %collective-permute-done.21), channel_id=1, source_target_pairs={{2,6},{5,7},{10,14},{13,15},{18,22},{21,23},{26,30},{29,31}} | collective-permute-start | bytes 2359304 | tf_op jit(solution)/shard_map/ppermute | solution.py:325
  46.9 14.2 %collective-permute-start.13 = (f32[2,256,256]{2,1,0:T(8,128)}, f32[2,256,256]{2,1,0:T(8,128)}, u32[]{:S(2)}, u32[]{:S(2)}) collective-permute-start(f32[2,256,256]{2,1,0:T(8,128)} %pick.1), channel_id=1, source_target_pairs={{0,2},{1,5},{8,10},{9,13},{16,18},{17,21},{24,26},{25,29}} | collective-permute-start | bytes 1572872 | tf_op jit(solution)/shard_map/ppermute | solution.py:325
  48.2 17.6 %collective-permute-start.5 = (f32[3,256,256]{2,1,0:T(8,128)}, f32[3,256,256]{2,1,0:T(8,128)}, u32[]{:S(2)}, u32[]{:S(2)}) collective-permute-start(f32[3,256,256]{2,1,0:T(8,128)} %collective-permute-done.4), channel_id=1, source_target_pairs={{2,6},{5,7},{10,14},{13,15},{18,22},{21,23},{26,30},{29,31}} | collective-permute-start | bytes 2359304 | tf_op jit(solution)/shard_map/ppermute | solution.py:325
  55.2 18.2 %collective-permute-start.26 = (f32[3,256,256]{2,1,0:T(8,128)}, f32[3,256,256]{2,1,0:T(8,128)}, u32[]{:S(2)}, u32[]{:S(2)}) collective-permute-start(f32[3,256,256]{2,1,0:T(8,128)} %collective-permute-done.25), channel_id=1, source_target_pairs={{2,6},{5,7},{10,14},{13,15},{18,22},{21,23},{26,30},{29,31}} | collective-permute-start | bytes 2359304 | tf_op jit(solution)/shard_map/ppermute | solution.py:325
  57.4 17.6 %collective-permute-start.2 = (f32[3,256,256]{2,1,0:T(8,128)}, f32[3,256,256]{2,1,0:T(8,128)}, u32[]{:S(2)}, u32[]{:S(2)}) collective-permute-start(f32[3,256,256]{2,1,0:T(8,128)} %collective-permute-done.1), channel_id=1, source_target_pairs={{6,4},{7,3},{14,12},{15,11},{22,20},{23,19},{30,28},{31,27}} | collective-permute-start | bytes 2359304 | tf_op jit(solution)/shard_map/ppermute | solution.py:325
  61.1 16.7 %collective-permute-start.18 = (f32[3,256,256]{2,1,0:T(8,128)S(1)}, f32[3,256,256]{2,1,0:T(8,128)S(1)}, u32[]{:S(2)}, u32[]{:S(2)}) collective-permute-start(f32[3,256,256]{2,1,0:T(8,128)S(1)} %collective-permute-done.17.refs_5_.refs_14_), channel_id=1, source_target_pairs={{8,16},{16,24},{9,17},{17,25},{10,18},{18,26},{11,19},{19,27},{12,... | collective-permute-start | bytes 2359304 | tf_op jit(solution)/shard_map/ppermute | solution.py:310
  64.2 15.6 %collective-permute-start.23 = (f32[3,256,256]{2,1,0:T(8,128)}, f32[3,256,256]{2,1,0:T(8,128)}, u32[]{:S(2)}, u32[]{:S(2)}) collective-permute-start(f32[3,256,256]{2,1,0:T(8,128)} %collective-permute-done.22), channel_id=1, source_target_pairs={{6,4},{7,3},{14,12},{15,11},{22,20},{23,19},{30,28},{31,27}} | collective-permute-start | bytes 2359304 | tf_op jit(solution)/shard_map/ppermute | solution.py:325
  65.8 13.3 %collective-permute-start.14 = (f32[2,256,256]{2,1,0:T(8,128)}, f32[2,256,256]{2,1,0:T(8,128)}, u32[]{:S(2)}, u32[]{:S(2)}) collective-permute-start(f32[2,256,256]{2,1,0:T(8,128)} %collective-permute-done.13), channel_id=1, source_target_pairs={{2,6},{5,7},{10,14},{13,15},{18,22},{21,23},{26,30},{29,31}} | collective-permute-start | bytes 1572872 | tf_op jit(solution)/shard_map/ppermute | solution.py:325
  75.0 16.8 %collective-permute-start.27 = (f32[3,256,256]{2,1,0:T(8,128)}, f32[3,256,256]{2,1,0:T(8,128)S(1)}, u32[]{:S(2)}, u32[]{:S(2)}) collective-permute-start(f32[3,256,256]{2,1,0:T(8,128)} %collective-permute-done.26), channel_id=1, source_target_pairs={{6,4},{7,3},{14,12},{15,11},{22,20},{23,19},{30,28},{31,27}} | collective-permute-start | bytes 2359304 | tf_op jit(solution)/shard_map/ppermute | solution.py:325
  77.7 22.5 %collective-permute-start.20 = (f32[3,256,256]{2,1,0:T(8,128)}, f32[3,256,256]{2,1,0:T(8,128)S(1)}, u32[]{:S(2)}, u32[]{:S(2)}) collective-permute-start(f32[3,256,256]{2,1,0:T(8,128)} %rows.1.refs_4_.refs_13_), channel_id=1, source_target_pairs={{8,0},{9,1},{10,2},{11,3},{12,4},{13,5},{14,6},{15,7}} | collective-permute-start | bytes 2359304 | tf_op jit(solution)/shard_map/ppermute | solution.py:304
  79.1 26.6 %collective-permute-start.19 = (f32[3,256,256]{2,1,0:T(8,128)S(1)}, f32[3,256,256]{2,1,0:T(8,128)S(1)}, u32[]{:S(2)}, u32[]{:S(2)}) collective-permute-start(f32[3,256,256]{2,1,0:T(8,128)S(1)} %collective-permute-done.18.refs_6_.refs_15_), channel_id=1, source_target_pairs={{16,24},{17,25},{18,26},{19,27},{20,28},{21,29},{22,30},{23,31}} | collective-permute-start | bytes 2359304 | tf_op jit(solution)/shard_map/ppermute | solution.py:310
  79.8 20.5 %collective-permute-start.15 = (f32[2,256,256]{2,1,0:T(8,128)}, f32[2,256,256]{2,1,0:T(8,128)S(1)}, u32[]{:S(2)}, u32[]{:S(2)}) collective-permute-start(f32[2,256,256]{2,1,0:T(8,128)} %collective-permute-done.14), channel_id=1, source_target_pairs={{6,4},{7,3},{14,12},{15,11},{22,20},{23,19},{30,28},{31,27}} | collective-permute-start | bytes 1572872 | tf_op jit(solution)/shard_map/ppermute | solution.py:325
  81.9 39.3 %collective-permute-start.7 = (f32[3,256,256]{2,1,0:T(8,128)S(1)}, f32[3,256,256]{2,1,0:T(8,128)S(1)}, u32[]{:S(2)}, u32[]{:S(2)}) collective-permute-start(f32[3,256,256]{2,1,0:T(8,128)S(1)} %select_select_fusion.3.mine_a), channel_id=1, source_target_pairs={{0,1},{1,0},{2,3},{3,2},{4,5},{5,4},{6,7},{7,6},{8,9},{9,8},{10,11... | collective-permute-start | bytes 2359304 | tf_op jit(solution)/shard_map/ppermute | solution.py:329
  91.8 22.7 %collective-permute-start.28 = (f32[3,256,256]{2,1,0:T(8,128)S(1)}, f32[3,256,256]{2,1,0:T(8,128)S(1)}, u32[]{:S(2)}, u32[]{:S(2)}) collective-permute-start(f32[3,256,256]{2,1,0:T(8,128)S(1)} %select_select_fusion.1.mine_a), channel_id=1, source_target_pairs={{0,1},{1,0},{2,3},{3,2},{4,5},{5,4},{6,7},{7,6},{8,9},{9,8},{10,11... | collective-permute-start | bytes 2359304 | tf_op jit(solution)/shard_map/ppermute | solution.py:329
  100.2 21.0 %collective-permute-start.8 = (f32[3,256,256]{2,1,0:T(8,128)S(1)}, f32[3,256,256]{2,1,0:T(8,128)S(1)}, u32[]{:S(2)}, u32[]{:S(2)}) collective-permute-start(f32[3,256,256]{2,1,0:T(8,128)S(1)} %select_select_fusion.2.mine_b), channel_id=1, source_target_pairs={{0,1},{1,0},{2,3},{3,2},{4,5},{5,4},{6,7},{7,6},{8,9},{9,8},{10,11... | collective-permute-start | bytes 2359304 | tf_op jit(solution)/shard_map/ppermute | solution.py:329
  100.3 14.3 %collective-permute-start.29 = (f32[3,256,256]{2,1,0:T(8,128)S(1)}, f32[3,256,256]{2,1,0:T(8,128)S(1)}, u32[]{:S(2)}, u32[]{:S(2)}) collective-permute-start(f32[3,256,256]{2,1,0:T(8,128)S(1)} %select_select_fusion.mine_b), channel_id=1, source_target_pairs={{0,1},{1,0},{2,3},{3,2},{4,5},{5,4},{6,7},{7,6},{8,9},{9,8},{10,11... | collective-permute-start | bytes 2359304 | tf_op jit(solution)/shard_map/ppermute | solution.py:329
  (20 other events, 668.2 us)
